TPU v7x, 128 devices: a whole 4x4x4 slice. The times are simulated.
128 devices in a mesh: dp: 1, tp: 16 (over z, y), pp: 8 (over x, core).
Axes of the slice: x: 4, y: 4, z: 4, core: 2. Of those that a mesh axis runs over, the one named last changes fastest.
Arguments:
- x_in: bfloat16 [2, 2, 512, 2560], P(None, 'dp', 'tp')
- ln_params: float32 [8, 4, 2560], P('pp')
- w_q: bfloat16 [8, 2560, 32, 1, 80], P('pp', None, 'tp')
- w_k: bfloat16 [8, 2560, 32, 80], P('pp', None, 'tp')
- w_v: bfloat16 [8, 2560, 32, 80], P('pp', None, 'tp')
- w_o: bfloat16 [8, 32, 1, 80, 2560], P('pp', 'tp')
- w_up: bfloat16 [8, 2560, 10240], P('pp', None, 'tp')
- w_down: bfloat16 [8, 10240, 2560], P('pp', 'tp')
Outputs:
- output: bfloat16 [8, 2, 2, 512, 2560], P('pp', None, 'dp', 'tp')
All inputs are finite; a program needn't handle non-finite values.
Results may differ from a plain program's by a relative error of at most 0.02.
Values are sent between devices in bfloat16 or wider.
A program may use at most 1 GiB of HBM per device.

v0:
```python
import jax
import jax.numpy as jnp
from jax import lax
from jax.sharding import PartitionSpec as P

LN_EPS = 1e-5
ROPE_BASE = 10000.0


def layer_norm(x_act, ln_gain, ln_bias):
    x_f32 = x_act.astype(jnp.float32)
    row_mean = jnp.mean(x_f32, axis=-1, keepdims=True)
    centred = x_f32 - row_mean
    variance = jnp.mean(centred * centred, axis=-1, keepdims=True)
    return (centred * lax.rsqrt(variance + LN_EPS) * ln_gain + ln_bias).astype(jnp.bfloat16)


def rope_tables(seq_len, head_dim):
    positions = jnp.arange(seq_len, dtype=jnp.float32)
    inv_freq = ROPE_BASE ** (-2.0 * jnp.arange(head_dim // 2, dtype=jnp.float32) / head_dim)
    angles = positions[:, None] * inv_freq[None, :]
    return jnp.cos(angles), jnp.sin(angles)


def apply_rope(proj, cos_tab, sin_tab):
    half_dim = proj.shape[-1] // 2
    table_shape = (1, proj.shape[1]) + (1,) * (proj.ndim - 3) + (half_dim,)
    cos_bcast = cos_tab.reshape(table_shape)
    sin_bcast = sin_tab.reshape(table_shape)
    first_half = proj[..., :half_dim]
    second_half = proj[..., half_dim:]
    return jnp.concatenate([first_half * cos_bcast - second_half * sin_bcast, second_half * cos_bcast + first_half * sin_bcast], axis=-1)


def causal_attention(q_proj, k_proj, v_proj):
    seq_len = q_proj.shape[1]
    scores = jnp.einsum("btkgh,bskh->bktgs", q_proj, k_proj, preferred_element_type=jnp.float32) * (q_proj.shape[-1] ** -0.5)
    positions = jnp.arange(seq_len)
    allowed = positions[:, None, None] >= positions[None, None, :]
    probs_bf = jax.nn.softmax(jnp.where(allowed, scores, -1e30), axis=-1).astype(jnp.bfloat16)
    return jnp.einsum("bktgs,bskh->bktgh", probs_bf, v_proj, preferred_element_type=jnp.float32).astype(jnp.bfloat16)


def branch_partial(x_full, ln_par, w_q, w_k, w_v, w_o, w_up, w_down):
    batch_dim, seq_len, d_model = x_full.shape
    kv_local, group_size, head_dim = w_q.shape[1:]
    num_rows = batch_dim * seq_len
    h_attn = layer_norm(x_full, ln_par[0], ln_par[1]).reshape(num_rows, d_model)
    h_mlp = layer_norm(x_full, ln_par[2], ln_par[3]).reshape(num_rows, d_model)
    cos_tab, sin_tab = rope_tables(seq_len, head_dim)
    q_proj = jnp.dot(h_attn, w_q.reshape(d_model, -1), preferred_element_type=jnp.float32)
    q_proj = apply_rope(q_proj.reshape(batch_dim, seq_len, kv_local, group_size, head_dim), cos_tab, sin_tab).astype(jnp.bfloat16)
    k_proj = jnp.dot(h_attn, w_k.reshape(d_model, -1), preferred_element_type=jnp.float32)
    k_proj = apply_rope(k_proj.reshape(batch_dim, seq_len, kv_local, head_dim), cos_tab, sin_tab).astype(jnp.bfloat16)
    v_proj = jnp.dot(h_attn, w_v.reshape(d_model, -1), preferred_element_type=jnp.float32).astype(jnp.bfloat16)
    v_proj = v_proj.reshape(batch_dim, seq_len, kv_local, head_dim)
    context = causal_attention(q_proj, k_proj, v_proj)
    attn_out = jnp.einsum("bktgh,kghd->btd", context, w_o, preferred_element_type=jnp.float32)
    hidden = jax.nn.gelu(jnp.dot(h_mlp, w_up, preferred_element_type=jnp.float32), approximate=False).astype(jnp.bfloat16)
    mlp_out = jnp.dot(hidden, w_down, preferred_element_type=jnp.float32).reshape(batch_dim, seq_len, d_model)
    return (attn_out + mlp_out).astype(jnp.bfloat16)


def solution(mesh):
    pp_size = mesh.shape["pp"]
    send_pairs = [(src_idx, src_idx + 1) for src_idx in range(pp_size - 1)]

    def stage_layer(x_shard, layer_weights):
        ln_par, wq_s, wk_s, wv_s, wo_s, wup_s, wdown_s = layer_weights
        x_full = lax.all_gather(x_shard, "tp", axis=1, tiled=True)
        partial_sum = branch_partial(x_full, ln_par, wq_s, wk_s, wv_s, wo_s, wup_s, wdown_s)
        reduced = lax.psum_scatter(partial_sum, "tp", scatter_dimension=1, tiled=True)
        return (x_shard.astype(jnp.float32) + reduced.astype(jnp.float32)).astype(jnp.bfloat16)

    def stage_body(x_in, ln_params, w_q, w_k, w_v, w_o, w_up, w_down):
        stage_idx = lax.axis_index("pp")
        num_micro = x_in.shape[0]
        layer_weights = (ln_params[0], w_q[0], w_k[0], w_v[0], w_o[0], w_up[0], w_down[0])

        def micro_step(step_idx, loop_carry):
            recv_buf, out_buf = loop_carry
            first_in = lax.dynamic_index_in_dim(x_in, jnp.minimum(step_idx, num_micro - 1), axis=0, keepdims=False)
            layer_in = jnp.where(stage_idx == 0, first_in, recv_buf)
            layer_out = stage_layer(layer_in, layer_weights)
            slot_idx = step_idx - stage_idx
            is_valid = (slot_idx >= 0) & (slot_idx < num_micro)
            slot_safe = jnp.clip(slot_idx, 0, num_micro - 1)
            previous = lax.dynamic_index_in_dim(out_buf, slot_safe, axis=0, keepdims=False)
            out_buf = lax.dynamic_update_index_in_dim(out_buf, jnp.where(is_valid, layer_out, previous), slot_safe, axis=0)
            recv_buf = lax.ppermute(layer_out, "pp", send_pairs)
            return recv_buf, out_buf

        init_carry = (jnp.zeros_like(x_in[0]), jnp.zeros_like(x_in))
        _, out_buf = lax.fori_loop(0, num_micro + pp_size - 1, micro_step, init_carry)
        return out_buf[None]

    in_specs = (P(None, "dp", "tp", None), P("pp", None, None), P("pp", None, "tp", None, None), P("pp", None, "tp", None), P("pp", None, "tp", None), P("pp", "tp", None, None, None), P("pp", None, "tp"), P("pp", "tp", None))
    return jax.shard_map(stage_body, mesh=mesh, in_specs=in_specs, out_specs=P("pp", None, "dp", "tp", None), check_vma=False)
```

profile of v0, /device:TPU:7, one launch (start us, length us, event | category | flops | bytes accessed | tf_op | source)
XLA Modules:
  0.0 1836.2 jit_solution(12349488123988624750)
XLA Ops:
  6.6 1821.9 %while.17 = (s32[]{:T(128)}, bf16[2,32,2560]{2,1,0:T(8,128)(2,1)S(1)}, bf16[2,2,32,2560]{3,2,1,0:T(8,128)(2,1)S(1)}, pred[]{:T(512)}, bf16[2,2,32,2560]{3,2,1,0:...) while((s32[]{:T(128)}, ...), condition=%wide.region_6.7_spmd, body=%wide.region_0.6_spmd.sunk | while | flops 10499545088 | bytes 213398448 | solution.py:94
  10.0 57.7 %all-gather.2.cloned.1.call-done = bf16[2,512,2560]{2,1,0:T(8,128)(2,1)} async-done(((bf16[2,32,2560]{2,1,0:T(8,128)(2,1)}), bf16[2,512,2560]{2,1,0:T(8,128)(2,1)}) %all-gather.2.cloned.1.call-update) | async-done | bytes 5242896 | tf_op jit(solution)/shard_map/while/body/eval_jaxpr/all_gather | solution.py:70
  89.4 22.1 %fusion.157 = f32[1024,2560]{1,0:T(8,128)} fusion(bf16[640,2560]{1,0:T(8,128)(2,1)} %get-tuple-element.507, bf16[1024,2560]{1,0:T(8,128)(2,1)} %bitcast.107, bf16[2560,640]{1,0:T(8,128)(2,1)} %get-tuple-element.506), kind=kOutput, calls=%fused_computation.45.clone.1 | convolution fusion | flops 6753484800 | bytes 22282240 | tf_op jit(solution)/shard_map/while/body/eval_jaxpr/dot_general | solution.py:60
  123.4 77.7 %reduce-scatter.2.cloned.1.call-done = bf16[2,32,2560]{2,1,0:T(8,128)(2,1)} async-done(((bf16[2,512,2560]{2,1,0:T(8,128)(2,1)}), bf16[2,32,2560]{2,1,0:T(8,128)(2,1)}) %reduce-scatter.2.cloned.1.call-update) | async-done | bytes 327696 | tf_op jit(solution)/shard_map/while/body/eval_jaxpr/reduce_scatter | solution.py:72
  211.2 59.2 %all-gather.2.cloned.1.call-done = bf16[2,512,2560]{2,1,0:T(8,128)(2,1)} async-done(((bf16[2,32,2560]{2,1,0:T(8,128)(2,1)}), bf16[2,512,2560]{2,1,0:T(8,128)(2,1)}) %all-gather.2.cloned.1.call-update) | async-done | bytes 5242896 | tf_op jit(solution)/shard_map/while/body/eval_jaxpr/all_gather | solution.py:70
  292.2 22.1 %fusion.157 = f32[1024,2560]{1,0:T(8,128)} fusion(bf16[640,2560]{1,0:T(8,128)(2,1)} %get-tuple-element.507, bf16[1024,2560]{1,0:T(8,128)(2,1)} %bitcast.107, bf16[2560,640]{1,0:T(8,128)(2,1)} %get-tuple-element.506), kind=kOutput, calls=%fused_computation.45.clone.1 | convolution fusion | flops 6753484800 | bytes 22282240 | tf_op jit(solution)/shard_map/while/body/eval_jaxpr/dot_general | solution.py:60
  326.2 77.7 %reduce-scatter.2.cloned.1.call-done = bf16[2,32,2560]{2,1,0:T(8,128)(2,1)} async-done(((bf16[2,512,2560]{2,1,0:T(8,128)(2,1)}), bf16[2,32,2560]{2,1,0:T(8,128)(2,1)}) %reduce-scatter.2.cloned.1.call-update) | async-done | bytes 327696 | tf_op jit(solution)/shard_map/while/body/eval_jaxpr/reduce_scatter | solution.py:72
  414.0 58.9 %all-gather.2.cloned.1.call-done = bf16[2,512,2560]{2,1,0:T(8,128)(2,1)} async-done(((bf16[2,32,2560]{2,1,0:T(8,128)(2,1)}), bf16[2,512,2560]{2,1,0:T(8,128)(2,1)}) %all-gather.2.cloned.1.call-update) | async-done | bytes 5242896 | tf_op jit(solution)/shard_map/while/body/eval_jaxpr/all_gather | solution.py:70
  494.6 22.1 %fusion.157 = f32[1024,2560]{1,0:T(8,128)} fusion(bf16[640,2560]{1,0:T(8,128)(2,1)} %get-tuple-element.507, bf16[1024,2560]{1,0:T(8,128)(2,1)} %bitcast.107, bf16[2560,640]{1,0:T(8,128)(2,1)} %get-tuple-element.506), kind=kOutput, calls=%fused_computation.45.clone.1 | convolution fusion | flops 6753484800 | bytes 22282240 | tf_op jit(solution)/shard_map/while/body/eval_jaxpr/dot_general | solution.py:60
  528.7 77.5 %reduce-scatter.2.cloned.1.call-done = bf16[2,32,2560]{2,1,0:T(8,128)(2,1)} async-done(((bf16[2,512,2560]{2,1,0:T(8,128)(2,1)}), bf16[2,32,2560]{2,1,0:T(8,128)(2,1)}) %reduce-scatter.2.cloned.1.call-update) | async-done | bytes 327696 | tf_op jit(solution)/shard_map/while/body/eval_jaxpr/reduce_scatter | solution.py:72
  616.3 59.3 %all-gather.2.cloned.1.call-done = bf16[2,512,2560]{2,1,0:T(8,128)(2,1)} async-done(((bf16[2,32,2560]{2,1,0:T(8,128)(2,1)}), bf16[2,512,2560]{2,1,0:T(8,128)(2,1)}) %all-gather.2.cloned.1.call-update) | async-done | bytes 5242896 | tf_op jit(solution)/shard_map/while/body/eval_jaxpr/all_gather | solution.py:70
  697.2 22.1 %fusion.157 = f32[1024,2560]{1,0:T(8,128)} fusion(bf16[640,2560]{1,0:T(8,128)(2,1)} %get-tuple-element.507, bf16[1024,2560]{1,0:T(8,128)(2,1)} %bitcast.107, bf16[2560,640]{1,0:T(8,128)(2,1)} %get-tuple-element.506), kind=kOutput, calls=%fused_computation.45.clone.1 | convolution fusion | flops 6753484800 | bytes 22282240 | tf_op jit(solution)/shard_map/while/body/eval_jaxpr/dot_general | solution.py:60
  731.3 77.5 %reduce-scatter.2.cloned.1.call-done = bf16[2,32,2560]{2,1,0:T(8,128)(2,1)} async-done(((bf16[2,512,2560]{2,1,0:T(8,128)(2,1)}), bf16[2,32,2560]{2,1,0:T(8,128)(2,1)}) %reduce-scatter.2.cloned.1.call-update) | async-done | bytes 327696 | tf_op jit(solution)/shard_map/while/body/eval_jaxpr/reduce_scatter | solution.py:72
  818.9 59.2 %all-gather.2.cloned.1.call-done = bf16[2,512,2560]{2,1,0:T(8,128)(2,1)} async-done(((bf16[2,32,2560]{2,1,0:T(8,128)(2,1)}), bf16[2,512,2560]{2,1,0:T(8,128)(2,1)}) %all-gather.2.cloned.1.call-update) | async-done | bytes 5242896 | tf_op jit(solution)/shard_map/while/body/eval_jaxpr/all_gather | solution.py:70
  899.8 22.1 %fusion.157 = f32[1024,2560]{1,0:T(8,128)} fusion(bf16[640,2560]{1,0:T(8,128)(2,1)} %get-tuple-element.507, bf16[1024,2560]{1,0:T(8,128)(2,1)} %bitcast.107, bf16[2560,640]{1,0:T(8,128)(2,1)} %get-tuple-element.506), kind=kOutput, calls=%fused_computation.45.clone.1 | convolution fusion | flops 6753484800 | bytes 22282240 | tf_op jit(solution)/shard_map/while/body/eval_jaxpr/dot_general | solution.py:60
  933.8 77.7 %reduce-scatter.2.cloned.1.call-done = bf16[2,32,2560]{2,1,0:T(8,128)(2,1)} async-done(((bf16[2,512,2560]{2,1,0:T(8,128)(2,1)}), bf16[2,32,2560]{2,1,0:T(8,128)(2,1)}) %reduce-scatter.2.cloned.1.call-update) | async-done | bytes 327696 | tf_op jit(solution)/shard_map/while/body/eval_jaxpr/reduce_scatter | solution.py:72
  1021.6 59.2 %all-gather.2.cloned.1.call-done = bf16[2,512,2560]{2,1,0:T(8,128)(2,1)} async-done(((bf16[2,32,2560]{2,1,0:T(8,128)(2,1)}), bf16[2,512,2560]{2,1,0:T(8,128)(2,1)}) %all-gather.2.cloned.1.call-update) | async-done | bytes 5242896 | tf_op jit(solution)/shard_map/while/body/eval_jaxpr/all_gather | solution.py:70
  1136.6 77.7 %reduce-scatter.2.cloned.1.call-done = bf16[2,32,2560]{2,1,0:T(8,128)(2,1)} async-done(((bf16[2,512,2560]{2,1,0:T(8,128)(2,1)}), bf16[2,32,2560]{2,1,0:T(8,128)(2,1)}) %reduce-scatter.2.cloned.1.call-update) | async-done | bytes 327696 | tf_op jit(solution)/shard_map/while/body/eval_jaxpr/reduce_scatter | solution.py:72
  1224.4 59.2 %all-gather.2.cloned.1.call-done = bf16[2,512,2560]{2,1,0:T(8,128)(2,1)} async-done(((bf16[2,32,2560]{2,1,0:T(8,128)(2,1)}), bf16[2,512,2560]{2,1,0:T(8,128)(2,1)}) %all-gather.2.cloned.1.call-update) | async-done | bytes 5242896 | tf_op jit(solution)/shard_map/while/body/eval_jaxpr/all_gather | solution.py:70
  1339.4 77.7 %reduce-scatter.2.cloned.1.call-done = bf16[2,32,2560]{2,1,0:T(8,128)(2,1)} async-done(((bf16[2,512,2560]{2,1,0:T(8,128)(2,1)}), bf16[2,32,2560]{2,1,0:T(8,128)(2,1)}) %reduce-scatter.2.cloned.1.call-update) | async-done | bytes 327696 | tf_op jit(solution)/shard_map/while/body/eval_jaxpr/reduce_scatter | solution.py:72
  1427.2 58.9 %all-gather.2.cloned.1.call-done = bf16[2,512,2560]{2,1,0:T(8,128)(2,1)} async-done(((bf16[2,32,2560]{2,1,0:T(8,128)(2,1)}), bf16[2,512,2560]{2,1,0:T(8,128)(2,1)}) %all-gather.2.cloned.1.call-update) | async-done | bytes 5242896 | tf_op jit(solution)/shard_map/while/body/eval_jaxpr/all_gather | solution.py:70
  1541.9 77.5 %reduce-scatter.2.cloned.1.call-done = bf16[2,32,2560]{2,1,0:T(8,128)(2,1)} async-done(((bf16[2,512,2560]{2,1,0:T(8,128)(2,1)}), bf16[2,32,2560]{2,1,0:T(8,128)(2,1)}) %reduce-scatter.2.cloned.1.call-update) | async-done | bytes 327696 | tf_op jit(solution)/shard_map/while/body/eval_jaxpr/reduce_scatter | solution.py:72
  1629.4 58.9 %all-gather.2.cloned.1.call-done = bf16[2,512,2560]{2,1,0:T(8,128)(2,1)} async-done(((bf16[2,32,2560]{2,1,0:T(8,128)(2,1)}), bf16[2,512,2560]{2,1,0:T(8,128)(2,1)}) %all-gather.2.cloned.1.call-update) | async-done | bytes 5242896 | tf_op jit(solution)/shard_map/while/body/eval_jaxpr/all_gather | solution.py:70
  1744.1 77.7 %reduce-scatter.2.cloned.1.call-done = bf16[2,32,2560]{2,1,0:T(8,128)(2,1)} async-done(((bf16[2,512,2560]{2,1,0:T(8,128)(2,1)}), bf16[2,32,2560]{2,1,0:T(8,128)(2,1)}) %reduce-scatter.2.cloned.1.call-update) | async-done | bytes 327696 | tf_op jit(solution)/shard_map/while/body/eval_jaxpr/reduce_scatter | solution.py:72
  (386 shorter events, 481.4 us)
Async XLA Ops:
  6.6 61.1 %all-gather.2.cloned.1.call-start = ((), (), s32[]{:S(2)}) async-start(), calls=%async_computation.1 | async-start | bytes 5570560 | tf_op jit(solution)/shard_map/while/body/eval_jaxpr/all_gather | solution.py:70
  8.4 192.7 %reduce-scatter.2.cloned.1.call-start = ((), (), s32[]{:S(2)}) async-start(), calls=%async_computation.2 | async-start | bytes 5570560 | tf_op jit(solution)/shard_map/while/body/eval_jaxpr/reduce_scatter | solution.py:72
  202.3 5.6 collective-permute-start
  207.9 62.6 %all-gather.2.cloned.1.call-start = ((), (), s32[]{:S(2)}) async-start(), calls=%async_computation.1 | async-start | bytes 5570560 | tf_op jit(solution)/shard_map/while/body/eval_jaxpr/all_gather | solution.py:70
  209.7 194.3 %reduce-scatter.2.cloned.1.call-start = ((), (), s32[]{:S(2)}) async-start(), calls=%async_computation.2 | async-start | bytes 5570560 | tf_op jit(solution)/shard_map/while/body/eval_jaxpr/reduce_scatter | solution.py:72
  405.0 5.6 collective-permute-start
  410.7 62.3 %all-gather.2.cloned.1.call-start = ((), (), s32[]{:S(2)}) async-start(), calls=%async_computation.1 | async-start | bytes 5570560 | tf_op jit(solution)/shard_map/while/body/eval_jaxpr/all_gather | solution.py:70
  412.4 193.7 %reduce-scatter.2.cloned.1.call-start = ((), (), s32[]{:S(2)}) async-start(), calls=%async_computation.2 | async-start | bytes 5570560 | tf_op jit(solution)/shard_map/while/body/eval_jaxpr/reduce_scatter | solution.py:72
  607.3 5.7 collective-permute-start
  612.9 62.6 %all-gather.2.cloned.1.call-start = ((), (), s32[]{:S(2)}) async-start(), calls=%async_computation.1 | async-start | bytes 5570560 | tf_op jit(solution)/shard_map/while/body/eval_jaxpr/all_gather | solution.py:70
  614.7 194.1 %reduce-scatter.2.cloned.1.call-start = ((), (), s32[]{:S(2)}) async-start(), calls=%async_computation.2 | async-start | bytes 5570560 | tf_op jit(solution)/shard_map/while/body/eval_jaxpr/reduce_scatter | solution.py:72
  809.9 5.6 collective-permute-start
  815.5 62.6 %all-gather.2.cloned.1.call-start = ((), (), s32[]{:S(2)}) async-start(), calls=%async_computation.1 | async-start | bytes 5570560 | tf_op jit(solution)/shard_map/while/body/eval_jaxpr/all_gather | solution.py:70
  817.3 194.3 %reduce-scatter.2.cloned.1.call-start = ((), (), s32[]{:S(2)}) async-start(), calls=%async_computation.2 | async-start | bytes 5570560 | tf_op jit(solution)/shard_map/while/body/eval_jaxpr/reduce_scatter | solution.py:72
  1018.3 62.6 %all-gather.2.cloned.1.call-start = ((), (), s32[]{:S(2)}) async-start(), calls=%async_computation.1 | async-start | bytes 5570560 | tf_op jit(solution)/shard_map/while/body/eval_jaxpr/all_gather | solution.py:70
  1020.1 194.3 %reduce-scatter.2.cloned.1.call-start = ((), (), s32[]{:S(2)}) async-start(), calls=%async_computation.2 | async-start | bytes 5570560 | tf_op jit(solution)/shard_map/while/body/eval_jaxpr/reduce_scatter | solution.py:72
  1221.1 62.6 %all-gather.2.cloned.1.call-start = ((), (), s32[]{:S(2)}) async-start(), calls=%async_computation.1 | async-start | bytes 5570560 | tf_op jit(solution)/shard_map/while/body/eval_jaxpr/all_gather | solution.py:70
  1222.8 194.3 %reduce-scatter.2.cloned.1.call-start = ((), (), s32[]{:S(2)}) async-start(), calls=%async_computation.2 | async-start | bytes 5570560 | tf_op jit(solution)/shard_map/while/body/eval_jaxpr/reduce_scatter | solution.py:72
  1418.2 5.6 collective-permute-start
  1423.9 62.3 %all-gather.2.cloned.1.call-start = ((), (), s32[]{:S(2)}) async-start(), calls=%async_computation.1 | async-start | bytes 5570560 | tf_op jit(solution)/shard_map/while/body/eval_jaxpr/all_gather | solution.py:70
  1425.6 193.7 %reduce-scatter.2.cloned.1.call-start = ((), (), s32[]{:S(2)}) async-start(), calls=%async_computation.2 | async-start | bytes 5570560 | tf_op jit(solution)/shard_map/while/body/eval_jaxpr/reduce_scatter | solution.py:72
  1620.4 5.7 collective-permute-start
  1626.1 62.3 %all-gather.2.cloned.1.call-start = ((), (), s32[]{:S(2)}) async-start(), calls=%async_computation.1 | async-start | bytes 5570560 | tf_op jit(solution)/shard_map/while/body/eval_jaxpr/all_gather | solution.py:70
  1627.9 194.0 %reduce-scatter.2.cloned.1.call-start = ((), (), s32[]{:S(2)}) async-start(), calls=%async_computation.2 | async-start | bytes 5570560 | tf_op jit(solution)/shard_map/while/body/eval_jaxpr/reduce_scatter | solution.py:72
  (76 other events, 974.8 us)
Sparse Core Ops, SparseCore 0:
  9.6 58.0 all-gather.1
  123.5 77.6 reduce-scatter.1
  210.8 59.5 all-gather.1
  326.3 77.6 reduce-scatter.1
  413.3 59.5 all-gather.1
  528.7 77.3 reduce-scatter.1
  615.9 59.6 all-gather.1
  731.3 77.4 reduce-scatter.1
  818.5 59.5 all-gather.1
  933.9 77.6 reduce-scatter.1
  1021.2 59.5 all-gather.1
  1136.7 77.6 reduce-scatter.1
  1224.0 59.5 all-gather.1
  1339.5 77.6 reduce-scatter.1
  1426.5 59.5 all-gather.1
  1541.9 77.3 reduce-scatter.1
  1628.7 59.6 all-gather.1
  1744.2 77.5 reduce-scatter.1
where the time goes:
time: 1840 us
  waiting for transfers between devices  1270 us (69%)
  matrix products  379 us (21%)
  other arithmetic  122 us (7%)
  local copies, waits for them, and re-layouts  39.5 us (2%)
    reduce_scatter x9, waiting for transfers between devices, stage_layer(): lax.psum_scatter(partial_sum, 'tp', scatter_dimension=1, tiled=True)  699 us
    all_gather x9, waiting for transfers between devices, stage_layer(): x_full = lax.all_gather(x_shard, 'tp', axis=1, tiled=True)  531 us
    dot_general x9, matrix products, branch_partial(): jnp.dot(hidden, w_down, preferred_element_type=jnp.float32)  199 us
    dot_general x9, matrix products, branch_partial(): jnp.einsum('bktgh,kghd->btd', context, w_o, preferred_element_type=jnp.fl...  73.3 us
    convert_element_type x9, other arithmetic, layer_norm(): (centred * lax.rsqrt(variance + LN_EPS) * ln_gain + ln_bias).astype(jnp.b...  46.5 us
    dot_general x9, matrix products, branch_partial(): jnp.dot(h_attn, w_q.reshape(d_model, -1), preferred_element_type=jnp.floa...  40.2 us
    ppermute x9, waiting for transfers between devices, micro_step(): recv_buf = lax.ppermute(layer_out, 'pp', send_pairs)  39 us
  transfers between devices with their start and end apart: 27, of which 27 were waited for; matrix products, arithmetic and copies ran while one was open for 1% of the time, Pallas kernels for 0%

commit v1 on v0

v1 whole, which is shorter than its diff:
```python
import functools

import jax
import jax.numpy as jnp
import numpy as np
from jax import lax
from jax.experimental import pallas as pl
from jax.experimental.pallas import tpu as pltpu
from jax.sharding import PartitionSpec as P

MESH = pl.DeviceIdType.MESH
LN_EPS = 1e-5
ROPE_BASE = 10000.0
F32, BF16 = jnp.float32, jnp.bfloat16

R = 4
BLK = 32
SEQ = R * R * BLK
D = 2560
HALF = D // 2
HEADS = 2
HD = 80
HH = HD // 2
FF = 640
QKV = 3 * HEADS * HD
ACT = FF + HEADS * HD
CHUNKS = 4


def rope_tables():
    positions = np.arange(SEQ, dtype=np.float32)
    inv_freq = (np.float32(ROPE_BASE) ** (np.float32(-2.0) * np.arange(HH, dtype=np.float32) / np.float32(HD))).astype(np.float32)
    angles = (inv_freq[:, None] * positions[None, :]).astype(np.float32)
    return np.cos(angles).astype(np.float32), np.sin(angles).astype(np.float32)


def nt_dot(a, b):
    return lax.dot_general(a, b, (((1,), (1,)), ((), ())), preferred_element_type=F32)


def nn_dot(a, b):
    return lax.dot_general(a, b, (((1,), (0,)), ((), ())), preferred_element_type=F32)


def kernel(pp_size, x_ref, ln_ref, wq_ref, wk_ref, wv_ref, wo_ref, wup_ref, wdown_ref, cos_ref, sin_ref, out_ref,
           xg, wqkv, wup, wcat, ha, hm, qv, ks, act, part, r1a, r1b, ma, mb, r2a, r2b, ybuf,
           w_sem, in_sem, out_sem, hop_send, hop_recv, g1_send, g1_recv, g2_send, g2_recv,
           s1a_send, s1a_recv, s1b_send, s1b_recv, s2_send, s2_recv):
    tp = lax.axis_index("tp")
    stage = lax.axis_index("pp")
    z, y = lax.div(tp, R), lax.rem(tp, R)
    last = pp_size - 1
    lo, hi = pl.ds(0, HALF), pl.ds(HALF, HALF)

    def row_peer(d):
        return {"tp": z * R + lax.rem(y + d, R)}

    def col_peer(d):
        return {"tp": lax.rem(z + d, R) * R + y}

    def remote(src, dst, send, recv, device):
        return pltpu.make_async_remote_copy(src_ref=src, dst_ref=dst, send_sem=send, recv_sem=recv, device_id=device, device_id_type=MESH)

    barrier = pltpu.get_barrier_semaphore()
    for d in (1, 2, 3):
        pl.semaphore_signal(barrier, inc=1, device_id=row_peer(d), device_id_type=MESH)
        pl.semaphore_signal(barrier, inc=1, device_id=col_peer(d), device_id_type=MESH)

    @pl.when(stage > 0)
    def _():
        pl.semaphore_signal(barrier, inc=1, device_id={"pp": stage - 1}, device_id_type=MESH)

    @pl.when(stage < last)
    def _():
        pl.semaphore_signal(barrier, inc=1, device_id={"pp": stage + 1}, device_id_type=MESH)

    nqk = HEADS * HD
    weight_copies = [
        pltpu.make_async_copy(wq_ref, wqkv.at[pl.ds(0, nqk)], w_sem.at[0]),
        pltpu.make_async_copy(wk_ref, wqkv.at[pl.ds(nqk, nqk)], w_sem.at[1]),
        pltpu.make_async_copy(wv_ref, wqkv.at[pl.ds(2 * nqk, nqk)], w_sem.at[2]),
        pltpu.make_async_copy(wup_ref, wup, w_sem.at[3]),
        pltpu.make_async_copy(wdown_ref, wcat.at[pl.ds(0, FF)], w_sem.at[4]),
        pltpu.make_async_copy(wo_ref, wcat.at[pl.ds(FF, nqk)], w_sem.at[5]),
    ]

    def input_copy(c):
        return pltpu.make_async_copy(x_ref.at[lax.div(c, 2), lax.rem(c, 2)], xg.at[c, z, y], in_sem.at[c])

    @pl.when(stage == 0)
    def _():
        for c in range(CHUNKS):
            input_copy(c).start()

    for cp in weight_copies:
        cp.start()

    pl.semaphore_wait(barrier, 6 + jnp.where(stage > 0, 1, 0) + jnp.where(stage < last, 1, 0))

    def hop_copy(c):
        return remote(ybuf.at[c], xg.at[c, z, y], hop_send.at[c], hop_recv.at[c], {"pp": lax.rem(stage + 1, pp_size)})

    def out_copy(c):
        return pltpu.make_async_copy(ybuf.at[c], out_ref.at[lax.div(c, 2), lax.rem(c, 2)], out_sem.at[c])

    def gather1(c, h, d, zz, yy):
        view = xg.at[c, zz, yy, :, lo if h == 0 else hi]
        return remote(view, view, g1_send.at[h, d - 1], g1_recv.at[c, h, d - 1], row_peer(d) if h == 0 else col_peer(d))

    def gather2(c, h, d, k):
        view = xg.at[c, k, :, :, lo] if h == 0 else xg.at[c, :, k, :, hi]
        return remote(view, view, g2_send.at[h, d - 1], g2_recv.at[c, h, d - 1], col_peer(d) if h == 0 else row_peer(d))

    def scatter1a(c, d):
        return remote(part.at[lax.rem(z + d, R), :, :, lo], r1a.at[c, d - 1], s1a_send.at[d - 1], s1a_recv.at[c, d - 1], col_peer(d))

    def scatter1b(c, e, zz):
        return remote(part.at[zz, lax.rem(y + e, R), :, hi], r1b.at[c, e - 1, zz], s1b_send.at[e - 1, zz], s1b_recv.at[c, e - 1, zz], row_peer(e))

    def scatter2(c, h, d):
        if h == 0:
            return remote(ma.at[lax.rem(y + d, R)], r2a.at[c, d - 1], s2_send.at[0, d - 1], s2_recv.at[c, 0, d - 1], row_peer(d))
        return remote(mb.at[lax.rem(z + d, R)], r2b.at[c, d - 1], s2_send.at[1, d - 1], s2_recv.at[c, 1, d - 1], col_peer(d))

    def back(k, d):
        return lax.rem(k + R - d, R)

    def chunk(c, carry):
        @pl.when(stage == 0)
        def _():
            input_copy(c).wait()

        @pl.when(stage > 0)
        def _():
            hop_copy(c).wait_recv()

        for d in (2, 1, 3):
            gather1(c, 0, d, z, y).start()
            gather1(c, 1, d, z, y).start()
        for d in (1, 2, 3):
            gather1(c, 0, d, z, back(y, d)).wait_recv()
        for d in (2, 1, 3):
            gather2(c, 0, d, z).start()
        for d in (1, 2, 3):
            gather1(c, 1, d, back(z, d), y).wait_recv()
        for d in (2, 1, 3):
            gather2(c, 1, d, y).start()
        for d in (1, 2, 3):
            gather2(c, 0, d, back(z, d)).wait_recv()
            gather2(c, 1, d, back(y, d)).wait_recv()

        def norm(j, carry):
            for half in range(2):
                rows = pl.ds(half * 16, 16)
                x = xg[c, lax.div(j, R), lax.rem(j, R), rows, :].astype(F32)
                mean = jnp.sum(x, axis=-1, keepdims=True) * (1.0 / D)
                x = x - mean
                var = jnp.sum(x * x, axis=-1, keepdims=True) * (1.0 / D)
                x = x * lax.rsqrt(var + LN_EPS)
                dst = pl.ds(pl.multiple_of(j * BLK + half * 16, 16), 16)
                ha[dst, :] = (x * ln_ref[0:1, :] + ln_ref[1:2, :]).astype(BF16)
                hm[dst, :] = (x * ln_ref[2:3, :] + ln_ref[3:4, :]).astype(BF16)
            return carry

        lax.fori_loop(0, R * R, norm, 0)

        @pl.when(c == 0)
        def _():
            for cp in weight_copies:
                cp.wait()

        for tb in range(2):
            toks = pl.ds(tb * 256, 256)
            proj = nt_dot(wqkv[...], ha[toks, :])
            cos, sin = cos_ref[:, toks], sin_ref[:, toks]

            def rope(row):
                first, second = proj[row:row + HH], proj[row + HH:row + HD]
                return jnp.concatenate([first * cos - second * sin, second * cos + first * sin], axis=0)

            for hd in range(HEADS):
                qv[pl.ds(hd * HD, HD), toks] = rope(hd * HD).astype(BF16)
                ks[hd, toks, :] = rope(nqk + hd * HD).T.astype(BF16)
            qv[pl.ds(nqk, nqk), toks] = proj[2 * nqk:].astype(BF16)

        for qb in range(2):
            toks = pl.ds(qb * 256, 256)
            nk = (qb + 1) * 256
            ctx = []
            for hd in range(HEADS):
                scores = nn_dot(ks[hd, 0:nk, :], qv[pl.ds(hd * HD, HD), toks]) * (HD ** -0.5)
                key_pos = lax.broadcasted_iota(jnp.int32, (nk, 256), 0)
                query_pos = lax.broadcasted_iota(jnp.int32, (nk, 256), 1) + qb * 256
                scores = jnp.where(query_pos >= key_pos, scores, -1e30)
                top = jnp.max(scores, axis=0, keepdims=True)
                probs = jnp.exp(scores - top)
                total = jnp.sum(probs, axis=0, keepdims=True)
                probs = (probs * (1.0 / total)).astype(BF16)
                ctx.append(nn_dot(qv[pl.ds(nqk + hd * HD, HD), 0:nk], probs))
            act[toks, FF:ACT] = jnp.concatenate(ctx, axis=0).T.astype(BF16)

        def up(i, carry):
            rows = pl.ds(pl.multiple_of(i * 128, 128), 128)
            pre = nn_dot(hm[rows, :], wup[...])
            act[rows, 0:FF] = (0.5 * pre * (1.0 + lax.erf(pre * np.float32(0.5 ** 0.5)))).astype(BF16)
            return carry

        lax.fori_loop(0, R, up, 0)

        for g in (1, 2, 3, 0):
            zz = lax.rem(z + g, R)
            rows = pl.ds(pl.multiple_of(zz * (R * BLK), R * BLK), R * BLK)
            part[zz] = nn_dot(act[rows, :], wcat[...]).astype(BF16).reshape(R, BLK, D)
            if g:
                scatter1a(c, g).start()
            for e in (2, 1, 3):
                scatter1b(c, e, zz).start()

        for d in (1, 2, 3):
            scatter1a(c, d).wait_recv()
        for d in (2, 1, 3, 0):
            k = lax.rem(y + d, R)
            total = part[z, k, :, lo].astype(F32)
            for e in range(3):
                total += r1a[c, e, k].astype(F32)
            ma[k] = total.astype(BF16)
            if d:
                scatter2(c, 0, d).start()
        for e in (1, 2, 3):
            for k in range(R):
                scatter1b(c, e, k).wait_recv()
        for d in (2, 1, 3, 0):
            k = lax.rem(z + d, R)
            total = part[k, y, :, hi].astype(F32)
            for e in range(3):
                total += r1b[c, e, k].astype(F32)
            mb[k] = total.astype(BF16)
            if d:
                scatter2(c, 1, d).start()
        for d in (1, 2, 3):
            scatter2(c, 0, d).wait_recv()
            scatter2(c, 1, d).wait_recv()
        sum_lo = ma[y].astype(F32)
        sum_hi = mb[z].astype(F32)
        for e in range(3):
            sum_lo += r2a[c, e].astype(F32)
            sum_hi += r2b[c, e].astype(F32)
        ybuf[c, :, lo] = (xg[c, z, y, :, lo].astype(F32) + sum_lo).astype(BF16)
        ybuf[c, :, hi] = (xg[c, z, y, :, hi].astype(F32) + sum_hi).astype(BF16)

        @pl.when(stage < last)
        def _():
            hop_copy(c).start()

        out_copy(c).start()

        for d in (1, 2, 3):
            for h in range(2):
                gather1(c, h, d, z, y).wait_send()
                gather2(c, h, d, z if h == 0 else y).wait_send()
                scatter2(c, h, d).wait_send()
            scatter1a(c, d).wait_send()
            for k in range(R):
                scatter1b(c, d, k).wait_send()
        return carry

    lax.fori_loop(0, CHUNKS, chunk, 0)

    for c in range(CHUNKS):
        out_copy(c).wait()

        @pl.when(stage < last)
        def _():
            hop_copy(c).wait_send()


def solution(mesh):
    pp_size = mesh.shape["pp"]
    cos_tab, sin_tab = rope_tables()
    any_spec = pl.BlockSpec(memory_space=pl.ANY)
    vmem_spec = pl.BlockSpec(memory_space=pltpu.VMEM)
    dma = pltpu.SemaphoreType.DMA

    def body(x_in, ln_params, w_q, w_k, w_v, w_o, w_up, w_down):
        flat = HEADS * HD
        wq = jnp.transpose(w_q[0], (1, 2, 3, 0)).reshape(flat, D)
        wk = jnp.transpose(w_k[0], (1, 2, 0)).reshape(flat, D)
        wv = jnp.transpose(w_v[0], (1, 2, 0)).reshape(flat, D)
        wo = w_o[0].reshape(flat, D)
        out = pl.pallas_call(
            functools.partial(kernel, pp_size),
            out_shape=jax.ShapeDtypeStruct(x_in.shape, BF16),
            in_specs=[any_spec, vmem_spec] + [any_spec] * 6 + [vmem_spec, vmem_spec],
            out_specs=any_spec,
            scratch_shapes=[
                pltpu.VMEM((CHUNKS, R, R, BLK, D), BF16),
                pltpu.VMEM((QKV, D), BF16),
                pltpu.VMEM((D, FF), BF16),
                pltpu.VMEM((ACT, D), BF16),
                pltpu.VMEM((SEQ, D), BF16),
                pltpu.VMEM((SEQ, D), BF16),
                pltpu.VMEM((2 * flat, SEQ), BF16),
                pltpu.VMEM((HEADS, SEQ, HD), BF16),
                pltpu.VMEM((SEQ, ACT), BF16),
                pltpu.VMEM((R, R, BLK, D), BF16),
                pltpu.VMEM((CHUNKS, 3, R, BLK, HALF), BF16),
                pltpu.VMEM((CHUNKS, 3, R, BLK, HALF), BF16),
                pltpu.VMEM((R, BLK, HALF), BF16),
                pltpu.VMEM((R, BLK, HALF), BF16),
                pltpu.VMEM((CHUNKS, 3, BLK, HALF), BF16),
                pltpu.VMEM((CHUNKS, 3, BLK, HALF), BF16),
                pltpu.VMEM((CHUNKS, BLK, D), BF16),
                dma((6,)), dma((CHUNKS,)), dma((CHUNKS,)), dma((CHUNKS,)), dma((CHUNKS,)),
                dma((2, 3)), dma((CHUNKS, 2, 3)), dma((2, 3)), dma((CHUNKS, 2, 3)),
                dma((3,)), dma((CHUNKS, 3)), dma((3, R)), dma((CHUNKS, 3, R)),
                dma((2, 3)), dma((CHUNKS, 2, 3)),
            ],
            compiler_params=pltpu.CompilerParams(collective_id=1, has_side_effects=True, vmem_limit_bytes=62 * 2**20),
            name="pipeline",
        )(x_in, ln_params[0], wq, wk, wv, wo, w_up[0], w_down[0], jnp.asarray(cos_tab), jnp.asarray(sin_tab))
        return out[None]

    in_specs = (P(None, "dp", "tp", None), P("pp", None, None), P("pp", None, "tp", None, None), P("pp", None, "tp", None), P("pp", None, "tp", None), P("pp", "tp", None, None, None), P("pp", None, "tp"), P("pp", "tp", None))
    return jax.shard_map(body, mesh=mesh, in_specs=in_specs, out_specs=P("pp", None, "dp", "tp", None), check_vma=False)
```

time: 1840 us -> 585 us (0.32)
  waiting for transfers between devices: 1270 us -> 0 us
  Pallas kernels: 0 us -> 582 us
  matrix products: 379 us -> 0 us
  other arithmetic: 122 us -> 0 us
  local copies, waits for them, and re-layouts: 39.5 us -> 1.97 us
    reduce_scatter x9 -> x0, waiting for transfers between devices: 699 us -> none  [stage_layer(): lax.psum_scatter(partial_sum, 'tp', scatter_dimension=1, tiled=True)]
    pallas_call x0 -> x1, Pallas kernels: none -> 582 us  [body(): pl.pallas_call(functools.partial(kernel, pp_size), out_shape=jax.ShapeDty...]
    all_gather x9 -> x0, waiting for transfers between devices: 531 us -> none  [stage_layer(): x_full = lax.all_gather(x_shard, 'tp', axis=1, tiled=True)]
    dot_general x45 -> x0, matrix products: 345 us -> none  [the longest x9 199 us: branch_partial(): jnp.dot(hidden, w_down, preferred_element_type=jnp.float32)]
    convert_element_type x9 -> x0, other arithmetic: 46.5 us -> none  [layer_norm(): (centred * lax.rsqrt(variance + LN_EPS) * ln_gain + ln_bias).astype(jnp.b...]
    reduce_sum x18 -> x0, other arithmetic: 44 us -> none  [the longest x9 30.5 us: layer_norm(): row_mean = jnp.mean(x_f32, axis=-1, keepdims=True)]
    ppermute x9 -> x0, waiting for transfers between devices: 39 us -> none  [micro_step(): recv_buf = lax.ppermute(layer_out, 'pp', send_pairs)]
    sub x9 -> x0, matrix products: 33.4 us -> none  [causal_attention(): jax.nn.softmax(jnp.where(allowed, scores, -1e+30), axis=-1)]
  transfers between devices with their start and end apart: 27 -> 0, of which waited for: 27 -> 0; matrix products, arithmetic and copies ran while one was open for 1% -> 0% of each run, Pallas kernels for 0% -> 0%
where the time goes in v1:
time: 585 us; the launch traced here: 584 us
  Pallas kernels  582 us (99%)
    pallas_call x1, Pallas kernels, body(): pl.pallas_call(functools.partial(kernel, pp_size), out_shape=jax.ShapeDty...  582 us

profile of v1, /device:TPU:7, one launch (start us, length us, event | category | flops | bytes accessed | tf_op | source)
XLA Modules:
  0.0 584.3 jit_solution(12923814277692413289)
XLA Ops:
  0.0 582.4 %pipeline.1 = bf16[2,2,32,2560]{3,2,1,0:T(8,128)(2,1)} custom-call(bf16[2,2,32,2560]{3,2,1,0:T(8,128)(2,1)} %x_ref.1, f32[4,2560]{1,0:T(4,128)} %bitcast.27, bf16[160,2560]{1,0:T(8,128)(2,1)} %bitcast.23, bf16[160,2560]{1,0:T(8,128)(2,1)} %bitcast.24, bf16[160,2560]{1,0:T(8,128)(2,1)} %bitcast.25, bf16[160,2560]{1,0:T(8,128)(2,1)} %bitcast.26, ...), custom_call_target="tpu_custom_call" | custom-call | tf_op jit(solution)/shard_map/pipeline/pallas_call | solution.py:290
  582.4 2.0 copy.12

commit v2 on v1

v2 whole, which is shorter than its diff:
```python
import functools

import jax
import jax.numpy as jnp
import numpy as np
from jax import lax
from jax.experimental import pallas as pl
from jax.experimental.pallas import tpu as pltpu
from jax.sharding import PartitionSpec as P

MESH = pl.DeviceIdType.MESH
LN_EPS = 1e-5
ROPE_BASE = 10000.0
F32, BF16 = jnp.float32, jnp.bfloat16

R = 4
BLK = 32
SEQ = R * R * BLK
D = 2560
SUB = BLK // 2
GROUP = R * BLK
ORDER = (0, 1, 3, 2)
SIDE = (0, 1, 1, 0)
HEADS = 2
HD = 80
HH = HD // 2
FF = 640
QKV = 3 * HEADS * HD
ACT = FF + HEADS * HD
CHUNKS = 4


def rope_tables():
    positions = np.arange(SEQ, dtype=np.float32)
    inv_freq = (np.float32(ROPE_BASE) ** (np.float32(-2.0) * np.arange(HH, dtype=np.float32) / np.float32(HD))).astype(np.float32)
    angles = (inv_freq[:, None] * positions[None, :]).astype(np.float32)
    return np.cos(angles).astype(np.float32), np.sin(angles).astype(np.float32)


def nt_dot(a, b):
    return lax.dot_general(a, b, (((1,), (1,)), ((), ())), preferred_element_type=F32)


def nn_dot(a, b):
    return lax.dot_general(a, b, (((1,), (0,)), ((), ())), preferred_element_type=F32)


def kernel(pp_size, x_ref, ln_ref, wq_ref, wk_ref, wv_ref, wo_ref, wup_ref, wdown_ref, cos_ref, sin_ref, out_ref,
           xg, wqkv, wup, wcat, ha, hm, qv, ks, act, part, r1, r2, r3, mid, r4, ybuf,
           w_sem, in_sem, out_sem, hop_send, hop_recv, p1_send, p1_recv, p2_send, p2_recv, p3_send, p3_recv,
           q1_send, q1_recv, q2_send, q2_recv, q3_send, q3_recv):
    tp = lax.axis_index("tp")
    stage = lax.axis_index("pp")
    z, y = lax.div(tp, R), lax.rem(tp, R)
    last = pp_size - 1
    nqk = HEADS * HD

    home = ((z, y), (y, z))

    def at(h, v, u):
        return (v, u) if h == 0 else (u, v)

    def peer(h, dv, du):
        v, u = home[h]
        zz, yy = at(h, lax.rem(v + dv, R), lax.rem(u + du, R))
        return {"tp": zz * R + yy}

    def remote(src, dst, send, recv, device):
        return pltpu.make_async_remote_copy(src_ref=src, dst_ref=dst, send_sem=send, recv_sem=recv, device_id=device, device_id_type=MESH)

    barrier = pltpu.get_barrier_semaphore()
    for d in (1, 2, 3):
        for h in range(2):
            pl.semaphore_signal(barrier, inc=1, device_id=peer(h, 0, d), device_id_type=MESH)

    @pl.when(stage > 0)
    def _():
        pl.semaphore_signal(barrier, inc=1, device_id={"pp": stage - 1}, device_id_type=MESH)

    @pl.when(stage < last)
    def _():
        pl.semaphore_signal(barrier, inc=1, device_id={"pp": stage + 1}, device_id_type=MESH)

    weight_copies = [
        pltpu.make_async_copy(wq_ref, wqkv.at[pl.ds(0, nqk)], w_sem.at[0]),
        pltpu.make_async_copy(wk_ref, wqkv.at[pl.ds(nqk, nqk)], w_sem.at[1]),
        pltpu.make_async_copy(wv_ref, wqkv.at[pl.ds(2 * nqk, nqk)], w_sem.at[2]),
        pltpu.make_async_copy(wup_ref, wup, w_sem.at[3]),
        pltpu.make_async_copy(wdown_ref, wcat.at[pl.ds(0, FF)], w_sem.at[4]),
        pltpu.make_async_copy(wo_ref, wcat.at[pl.ds(FF, nqk)], w_sem.at[5]),
    ]

    def input_copy(c):
        return pltpu.make_async_copy(x_ref.at[lax.div(c, 2), lax.rem(c, 2)], xg.at[c, z, y], in_sem.at[c])

    @pl.when(stage == 0)
    def _():
        for c in range(CHUNKS):
            input_copy(c).start()

    for cp in weight_copies:
        cp.start()

    pl.semaphore_wait(barrier, 6 + jnp.where(stage > 0, 1, 0) + jnp.where(stage < last, 1, 0))

    def hop_copy(c):
        return remote(ybuf.at[c], xg.at[c, z, y], hop_send.at[c], hop_recv.at[c], {"pp": lax.rem(stage + 1, pp_size)})

    def out_copy(c):
        return pltpu.make_async_copy(ybuf.at[c], out_ref.at[lax.div(c, 2), lax.rem(c, 2)], out_sem.at[c])

    def place(h, dv, du):
        v, u = home[h]
        return at(h, lax.rem(v + dv + R, R), lax.rem(u + du + R, R))

    def gathered(c, h, dv, du):
        zz, yy = place(h, dv, du)
        return xg.at[c, zz, yy, pl.ds(h * SUB, SUB), :]

    def partial_at(h, dv, du):
        zz, yy = place(h, dv, du)
        return part.at[zz, yy, pl.ds(h * SUB, SUB), :]

    def p1(c, h, d, incoming=False):
        view = gathered(c, h, 0, -d if incoming else 0)
        return remote(view, view, p1_send.at[h, d - 1], p1_recv.at[c, h, d - 1], peer(h, 0, d))

    def p2(c, h, side, k, incoming=False):
        view = gathered(c, h, ((-1, 1)[side] if incoming else 0), -k)
        return remote(view, view, p2_send.at[h, side, k], p2_recv.at[c, h, side, k], peer(h, (1, R - 1)[side], 0))

    def p3(c, h, k, incoming=False):
        side = SIDE[k]
        view = gathered(c, h, (2 if incoming else (-1, 1)[side]), -k)
        return remote(view, view, p3_send.at[h, k], p3_recv.at[c, h, k], peer(h, (1, R - 1)[side], 0))

    def q1(c, h, k):
        return remote(partial_at(h, 2, -k), r1.at[c, h, k], q1_send.at[h, k], q1_recv.at[c, h, k], peer(h, (1, R - 1)[SIDE[k]], 0))

    def q2(c, h, side, k):
        return remote(partial_at(h, (1, -1)[side], -k), (r2 if side == 0 else r3).at[c, h, k], q2_send.at[h, side, k], q2_recv.at[c, h, side, k],
                      peer(h, (1, R - 1)[side], 0))

    def q3(c, h, k):
        return remote(mid.at[h, k], r4.at[c, h, k - 1], q3_send.at[h, k - 1], q3_recv.at[c, h, k - 1], peer(h, 0, R - k))

    def row_group(c, off):
        zz = lax.rem(z + off, R)
        base = pl.multiple_of(zz * GROUP, GROUP)
        toks = pl.ds(base, GROUP)

        def norm(j, carry):
            x = xg[c, zz, lax.div(j, 2), pl.ds(pl.multiple_of(lax.rem(j, 2) * SUB, SUB), SUB), :].astype(F32)
            mean = jnp.sum(x, axis=-1, keepdims=True) * (1.0 / D)
            x = x - mean
            var = jnp.sum(x * x, axis=-1, keepdims=True) * (1.0 / D)
            x = x * lax.rsqrt(var + LN_EPS)
            dst = pl.ds(pl.multiple_of(j * SUB, SUB), SUB)
            ha[dst, :] = (x * ln_ref[0:1, :] + ln_ref[1:2, :]).astype(BF16)
            hm[dst, :] = (x * ln_ref[2:3, :] + ln_ref[3:4, :]).astype(BF16)
            return carry

        lax.fori_loop(0, GROUP // SUB, norm, 0)

        if off == 0:
            @pl.when(c == 0)
            def _():
                for cp in weight_copies:
                    cp.wait()

        proj = nt_dot(wqkv[...], ha[...])
        cos, sin = cos_ref[:, toks], sin_ref[:, toks]

        def rope(row):
            first, second = proj[row:row + HH], proj[row + HH:row + HD]
            return jnp.concatenate([first * cos - second * sin, second * cos + first * sin], axis=0)

        for hd in range(HEADS):
            qv[pl.ds(hd * HD, HD), toks] = rope(hd * HD).astype(BF16)
            ks[hd, toks, :] = rope(nqk + hd * HD).T.astype(BF16)
        qv[pl.ds(nqk, nqk), toks] = proj[2 * nqk:].astype(BF16)

        pre = nn_dot(hm[...], wup[...])
        act[toks, 0:FF] = (0.5 * pre * (1.0 + lax.erf(pre * np.float32(0.5 ** 0.5)))).astype(BF16)

    def chunk(c, carry):
        @pl.when(stage == 0)
        def _():
            input_copy(c).wait()

        @pl.when(stage > 0)
        def _():
            hop_copy(c).wait_recv()

        for d in (1, 3, 2):
            for h in range(2):
                p1(c, h, d).start()
        for h in range(2):
            for side in range(2):
                p2(c, h, side, 0).start()
        for k in ORDER[1:]:
            for h in range(2):
                p1(c, h, k, True).wait_recv()
                for side in range(2):
                    p2(c, h, side, k).start()

        def forward(k):
            for h in range(2):
                p2(c, h, SIDE[k], k, True).wait_recv()
                p3(c, h, k).start()

        def others(h, side, ks_):
            for k in ks_:
                p2(c, h, side, k, True).wait_recv()

        forward(0)
        forward(1)
        others(1, 1, (0,))
        p3(c, 1, 0, True).wait_recv()
        row_group(c, 0)
        forward(3)
        forward(2)
        others(0, 0, (1, 2))
        others(1, 0, (1,))
        p3(c, 1, 1, True).wait_recv()
        row_group(c, 3)
        others(0, 1, (0, 3))
        others(1, 1, (3,))
        p3(c, 1, 3, True).wait_recv()
        row_group(c, 1)
        for k in ORDER:
            p3(c, 0, k, True).wait_recv()
        others(1, 0, (2,))
        p3(c, 1, 2, True).wait_recv()
        row_group(c, 2)

        for qb in range(2):
            toks = pl.ds(qb * 256, 256)
            nk = (qb + 1) * 256
            ctx = []
            for hd in range(HEADS):
                scores = nn_dot(ks[hd, 0:nk, :], qv[pl.ds(hd * HD, HD), toks]) * (HD ** -0.5)
                key_pos = lax.broadcasted_iota(jnp.int32, (nk, 256), 0)
                query_pos = lax.broadcasted_iota(jnp.int32, (nk, 256), 1) + qb * 256
                scores = jnp.where(query_pos >= key_pos, scores, -1e30)
                top = jnp.max(scores, axis=0, keepdims=True)
                probs = jnp.exp(scores - top)
                total = jnp.sum(probs, axis=0, keepdims=True)
                probs = (probs * (1.0 / total)).astype(BF16)
                ctx.append(nn_dot(qv[pl.ds(nqk + hd * HD, HD), 0:nk], probs))
            act[toks, FF:ACT] = jnp.concatenate(ctx, axis=0).T.astype(BF16)

        for off in (2, 3, 1, 0):
            zz = lax.rem(z + off, R)
            rows = pl.ds(pl.multiple_of(zz * GROUP, GROUP), GROUP)
            part[zz] = nn_dot(act[rows, :], wcat[...]).astype(BF16).reshape(R, BLK, D)
            k1 = (R - off) % R
            q1(c, 1, k1).start()
            if off == 2:
                for k in ORDER:
                    q1(c, 0, k).start()
            elif off == 3:
                for k in ORDER:
                    if SIDE[k] == 0:
                        q2(c, 0, 1, k).start()
            elif off == 1:
                for k in ORDER:
                    if SIDE[k] == 1:
                        q2(c, 0, 0, k).start()
            q2(c, 1, 1 - SIDE[k1], k1).start()

        for h, k in [(0, 0), (0, 1), (1, 2), (0, 3), (0, 2), (1, 1), (1, 3), (1, 0)]:
            side = SIDE[k]
            q1(c, h, k).wait_recv()
            mine = partial_at(h, (1, -1)[side], -k)
            mine[...] = (mine[...].astype(F32) + r1[c, h, k].astype(F32)).astype(BF16)
            q2(c, h, side, k).start()
        for k in (1, 2, 3, 0):
            for h in range(2):
                q2(c, h, 0, k).wait_recv()
                q2(c, h, 1, k).wait_recv()
                total = partial_at(h, 0, -k)[...].astype(F32) + r2[c, h, k].astype(F32) + r3[c, h, k].astype(F32)
                mid[h, k] = total.astype(BF16)
                if k:
                    q3(c, h, k).start()
        for h in range(2):
            rows = pl.ds(h * SUB, SUB)
            total = xg[c, z, y, rows, :].astype(F32) + mid[h, 0].astype(F32)
            for k in (1, 2, 3):
                q3(c, h, k).wait_recv()
                total += r4[c, h, k - 1].astype(F32)
            ybuf[c, rows, :] = total.astype(BF16)

        @pl.when(stage < last)
        def _():
            hop_copy(c).start()

        out_copy(c).start()

        for h in range(2):
            for k in range(R):
                if k:
                    p1(c, h, k).wait_send()
                    q3(c, h, k).wait_send()
                for side in range(2):
                    p2(c, h, side, k).wait_send()
                    q2(c, h, side, k).wait_send()
                p3(c, h, k).wait_send()
                q1(c, h, k).wait_send()
        return carry

    lax.fori_loop(0, CHUNKS, chunk, 0)

    for c in range(CHUNKS):
        out_copy(c).wait()

        @pl.when(stage < last)
        def _():
            hop_copy(c).wait_send()


def solution(mesh):
    pp_size = mesh.shape["pp"]
    cos_tab, sin_tab = rope_tables()
    any_spec = pl.BlockSpec(memory_space=pl.ANY)
    vmem_spec = pl.BlockSpec(memory_space=pltpu.VMEM)
    dma = pltpu.SemaphoreType.DMA

    def body(x_in, ln_params, w_q, w_k, w_v, w_o, w_up, w_down):
        flat = HEADS * HD
        wq = jnp.transpose(w_q[0], (1, 2, 3, 0)).reshape(flat, D)
        wk = jnp.transpose(w_k[0], (1, 2, 0)).reshape(flat, D)
        wv = jnp.transpose(w_v[0], (1, 2, 0)).reshape(flat, D)
        wo = w_o[0].reshape(flat, D)
        out = pl.pallas_call(
            functools.partial(kernel, pp_size),
            out_shape=jax.ShapeDtypeStruct(x_in.shape, BF16),
            in_specs=[any_spec, vmem_spec] + [any_spec] * 6 + [vmem_spec, vmem_spec],
            out_specs=any_spec,
            scratch_shapes=[
                pltpu.VMEM((CHUNKS, R, R, BLK, D), BF16),
                pltpu.VMEM((QKV, D), BF16),
                pltpu.VMEM((D, FF), BF16),
                pltpu.VMEM((ACT, D), BF16),
                pltpu.VMEM((GROUP, D), BF16),
                pltpu.VMEM((GROUP, D), BF16),
                pltpu.VMEM((2 * flat, SEQ), BF16),
                pltpu.VMEM((HEADS, SEQ, HD), BF16),
                pltpu.VMEM((SEQ, ACT), BF16),
                pltpu.VMEM((R, R, BLK, D), BF16),
                pltpu.VMEM((CHUNKS, 2, R, SUB, D), BF16),
                pltpu.VMEM((CHUNKS, 2, R, SUB, D), BF16),
                pltpu.VMEM((CHUNKS, 2, R, SUB, D), BF16),
                pltpu.VMEM((2, R, SUB, D), BF16),
                pltpu.VMEM((CHUNKS, 2, R - 1, SUB, D), BF16),
                pltpu.VMEM((CHUNKS, BLK, D), BF16),
                dma((6,)), dma((CHUNKS,)), dma((CHUNKS,)), dma((CHUNKS,)), dma((CHUNKS,)),
                dma((2, 3)), dma((CHUNKS, 2, 3)), dma((2, 2, R)), dma((CHUNKS, 2, 2, R)), dma((2, R)), dma((CHUNKS, 2, R)),
                dma((2, R)), dma((CHUNKS, 2, R)), dma((2, 2, R)), dma((CHUNKS, 2, 2, R)), dma((2, 3)), dma((CHUNKS, 2, 3)),
            ],
            compiler_params=pltpu.CompilerParams(collective_id=1, has_side_effects=True, vmem_limit_bytes=62 * 2**20),
            name="pipeline",
        )(x_in, ln_params[0], wq, wk, wv, wo, w_up[0], w_down[0], jnp.asarray(cos_tab), jnp.asarray(sin_tab))
        return out[None]

    in_specs = (P(None, "dp", "tp", None), P("pp", None, None), P("pp", None, "tp", None, None), P("pp", None, "tp", None), P("pp", None, "tp", None), P("pp", "tp", None, None, None), P("pp", None, "tp"), P("pp", "tp", None))
    return jax.shard_map(body, mesh=mesh, in_specs=in_specs, out_specs=P("pp", None, "dp", "tp", None), check_vma=False)
```

time: 585 us -> 535 us (0.915)
  Pallas kernels: 582 us -> 533 us
    pallas_call x1, Pallas kernels: 582 us -> 533 us  [body(): pl.pallas_call(functools.partial(kernel, pp_size), out_shape=jax.ShapeDty...]
where the time goes in v2:
time: 535 us
  Pallas kernels  533 us (100%)
    pallas_call x1, Pallas kernels, body(): pl.pallas_call(functools.partial(kernel, pp_size), out_shape=jax.ShapeDty...  533 us

profile of v2, /device:TPU:7, one launch (start us, length us, event | category | flops | bytes accessed | tf_op | source)
XLA Modules:
  0.0 534.9 jit_solution(8977850806173448536)
XLA Ops:
  0.0 532.9 %pipeline.1 = bf16[2,2,32,2560]{3,2,1,0:T(8,128)(2,1)} custom-call(bf16[2,2,32,2560]{3,2,1,0:T(8,128)(2,1)} %x_ref.1, f32[4,2560]{1,0:T(4,128)} %bitcast.27, bf16[160,2560]{1,0:T(8,128)(2,1)} %bitcast.23, bf16[160,2560]{1,0:T(8,128)(2,1)} %bitcast.24, bf16[160,2560]{1,0:T(8,128)(2,1)} %bitcast.25, bf16[160,2560]{1,0:T(8,128)(2,1)} %bitcast.26, ...), custom_call_target="tpu_custom_call" | custom-call | tf_op jit(solution)/shard_map/pipeline/pallas_call | solution.py:335
  532.9 2.0 copy.12

commit v3 on v2

--- a/solution.py
+++ b/solution.py
@@ -48,7 +48,7 @@
 def kernel(pp_size, x_ref, ln_ref, wq_ref, wk_ref, wv_ref, wo_ref, wup_ref, wdown_ref, cos_ref, sin_ref, out_ref,
            xg, wqkv, wup, wcat, ha, hm, qv, ks, act, part, r1, r2, r3, mid, r4, ybuf,
            w_sem, in_sem, out_sem, hop_send, hop_recv, p1_send, p1_recv, p2_send, p2_recv, p3_send, p3_recv,
-           q1_send, q1_recv, q2_send, q2_recv, q3_send, q3_recv):
+           q1_send, q1_recv, q2_send, q2_recv, q3_send, q3_recv, turn_sem):
     tp = lax.axis_index("tp")
     stage = lax.axis_index("pp")
     z, y = lax.div(tp, R), lax.rem(tp, R)
@@ -131,11 +131,11 @@
 
     def p3(c, h, k, incoming=False):
         side = SIDE[k]
-        view = gathered(c, h, (2 if incoming else (-1, 1)[side]), -k)
-        return remote(view, view, p3_send.at[h, k], p3_recv.at[c, h, k], peer(h, (1, R - 1)[side], 0))
+        view = gathered(c, h, 2 if incoming else (-1, 1)[side] if k else 0, -k)
+        return remote(view, view, p3_send.at[h, k], p3_recv.at[c, h, k], peer(h, (1, R - 1)[side] if k else 2, 0))
 
     def q1(c, h, k):
-        return remote(partial_at(h, 2, -k), r1.at[c, h, k], q1_send.at[h, k], q1_recv.at[c, h, k], peer(h, (1, R - 1)[SIDE[k]], 0))
+        return remote(partial_at(h, 2, -k), r1.at[c, h, k], q1_send.at[h, k], q1_recv.at[c, h, k], peer(h, (1, R - 1)[SIDE[k]] if k else 2, 0))
 
     def q2(c, h, side, k):
         return remote(partial_at(h, (1, -1)[side], -k), (r2 if side == 0 else r3).at[c, h, k], q2_send.at[h, side, k], q2_recv.at[c, h, side, k],
@@ -144,65 +144,67 @@
     def q3(c, h, k):
         return remote(mid.at[h, k], r4.at[c, h, k - 1], q3_send.at[h, k - 1], q3_recv.at[c, h, k - 1], peer(h, 0, R - k))
 
-    def row_group(c, off):
+    def norms(c, off, slot):
         zz = lax.rem(z + off, R)
-        base = pl.multiple_of(zz * GROUP, GROUP)
-        toks = pl.ds(base, GROUP)
-
-        def norm(j, carry):
-            x = xg[c, zz, lax.div(j, 2), pl.ds(pl.multiple_of(lax.rem(j, 2) * SUB, SUB), SUB), :].astype(F32)
-            mean = jnp.sum(x, axis=-1, keepdims=True) * (1.0 / D)
-            x = x - mean
-            var = jnp.sum(x * x, axis=-1, keepdims=True) * (1.0 / D)
-            x = x * lax.rsqrt(var + LN_EPS)
-            dst = pl.ds(pl.multiple_of(j * SUB, SUB), SUB)
-            ha[dst, :] = (x * ln_ref[0:1, :] + ln_ref[1:2, :]).astype(BF16)
-            hm[dst, :] = (x * ln_ref[2:3, :] + ln_ref[3:4, :]).astype(BF16)
-            return carry
-
-        lax.fori_loop(0, GROUP // SUB, norm, 0)
-
-        if off == 0:
-            @pl.when(c == 0)
+        for yy in range(R):
+            total = jnp.sum(xg[c, zz, yy].astype(F32), axis=-1, keepdims=True)
+            mean = total * (1.0 / D)
+            dev = xg[c, zz, yy].astype(F32) - mean
+            var = jnp.sum(dev * dev, axis=-1, keepdims=True) * (1.0 / D)
+            scale = lax.rsqrt(var + LN_EPS)
+            unit = (xg[c, zz, yy].astype(F32) - mean) * scale
+            dst = pl.ds(slot * GROUP + yy * BLK, BLK)
+            ha[dst, :] = (unit * ln_ref[0:1, :] + ln_ref[1:2, :]).astype(BF16)
+            hm[dst, :] = (unit * ln_ref[2:3, :] + ln_ref[3:4, :]).astype(BF16)
+
+    def project(offs):
+        toks = [pl.ds(pl.multiple_of(lax.rem(z + off, R) * GROUP, GROUP), GROUP) for off in offs]
+
+        proj = nt_dot(wqkv[...], ha[...])
+        for slot, tok in enumerate(toks):
+            cols = proj[:, slot * GROUP:(slot + 1) * GROUP]
+            cos, sin = cos_ref[:, tok], sin_ref[:, tok]
+
+            def rope(row):
+                first, second = cols[row:row + HH], cols[row + HH:row + HD]
+                return jnp.concatenate([first * cos - second * sin, second * cos + first * sin], axis=0)
+
+            for hd in range(HEADS):
+                qv[pl.ds(hd * HD, HD), tok] = rope(hd * HD).astype(BF16)
+                ks[hd, tok, :] = rope(nqk + hd * HD).T.astype(BF16)
+            qv[pl.ds(nqk, nqk), tok] = cols[2 * nqk:].astype(BF16)
+
+        for slot, tok in enumerate(toks):
+            pre = nn_dot(hm[slot * GROUP:(slot + 1) * GROUP, :], wup[...])
+            act[tok, 0:FF] = (0.5 * pre * (1.0 + lax.erf(pre * np.float32(0.5 ** 0.5)))).astype(BF16)
+
+    def chunk(c, carry):
+        with jax.named_scope("wait_in"):
+            @pl.when(stage == 0)
             def _():
-                for cp in weight_copies:
-                    cp.wait()
-
-        proj = nt_dot(wqkv[...], ha[...])
-        cos, sin = cos_ref[:, toks], sin_ref[:, toks]
-
-        def rope(row):
-            first, second = proj[row:row + HH], proj[row + HH:row + HD]
-            return jnp.concatenate([first * cos - second * sin, second * cos + first * sin], axis=0)
-
-        for hd in range(HEADS):
-            qv[pl.ds(hd * HD, HD), toks] = rope(hd * HD).astype(BF16)
-            ks[hd, toks, :] = rope(nqk + hd * HD).T.astype(BF16)
-        qv[pl.ds(nqk, nqk), toks] = proj[2 * nqk:].astype(BF16)
-
-        pre = nn_dot(hm[...], wup[...])
-        act[toks, 0:FF] = (0.5 * pre * (1.0 + lax.erf(pre * np.float32(0.5 ** 0.5)))).astype(BF16)
-
-    def chunk(c, carry):
-        @pl.when(stage == 0)
-        def _():
-            input_copy(c).wait()
-
-        @pl.when(stage > 0)
-        def _():
-            hop_copy(c).wait_recv()
-
-        for d in (1, 3, 2):
+                input_copy(c).wait()
+
+            @pl.when(stage > 0)
+            def _():
+                hop_copy(c).wait_recv()
+
+            @pl.when((c > 0) & (lax.rem(stage, 2) == 0))
+            def _():
+                pl.semaphore_wait(turn_sem, 1)
+
+        with jax.named_scope("p1_wait"):
             for h in range(2):
-                p1(c, h, d).start()
-        for h in range(2):
-            for side in range(2):
-                p2(c, h, side, 0).start()
-        for k in ORDER[1:]:
-            for h in range(2):
-                p1(c, h, k, True).wait_recv()
+                for d in (1, 3):
+                    p1(c, h, d).start()
                 for side in range(2):
-                    p2(c, h, side, k).start()
+                    p2(c, 1 - h, side, 0).start()
+                p1(c, h, 2).start()
+                p3(c, 1 - h, 0).start()
+            for k in ORDER[1:]:
+                for h in range(2):
+                    p1(c, h, k, True).wait_recv()
+                    for side in range(2):
+                        p2(c, h, side, k).start()
 
         def forward(k):
             for h in range(2):
@@ -213,83 +215,110 @@
             for k in ks_:
                 p2(c, h, side, k, True).wait_recv()
 
-        forward(0)
-        forward(1)
-        others(1, 1, (0,))
-        p3(c, 1, 0, True).wait_recv()
-        row_group(c, 0)
-        forward(3)
-        forward(2)
-        others(0, 0, (1, 2))
-        others(1, 0, (1,))
-        p3(c, 1, 1, True).wait_recv()
-        row_group(c, 3)
-        others(0, 1, (0, 3))
-        others(1, 1, (3,))
-        p3(c, 1, 3, True).wait_recv()
-        row_group(c, 1)
-        for k in ORDER:
-            p3(c, 0, k, True).wait_recv()
-        others(1, 0, (2,))
-        p3(c, 1, 2, True).wait_recv()
-        row_group(c, 2)
-
-        for qb in range(2):
-            toks = pl.ds(qb * 256, 256)
-            nk = (qb + 1) * 256
-            ctx = []
-            for hd in range(HEADS):
-                scores = nn_dot(ks[hd, 0:nk, :], qv[pl.ds(hd * HD, HD), toks]) * (HD ** -0.5)
-                key_pos = lax.broadcasted_iota(jnp.int32, (nk, 256), 0)
-                query_pos = lax.broadcasted_iota(jnp.int32, (nk, 256), 1) + qb * 256
-                scores = jnp.where(query_pos >= key_pos, scores, -1e30)
-                top = jnp.max(scores, axis=0, keepdims=True)
-                probs = jnp.exp(scores - top)
-                total = jnp.sum(probs, axis=0, keepdims=True)
-                probs = (probs * (1.0 / total)).astype(BF16)
-                ctx.append(nn_dot(qv[pl.ds(nqk + hd * HD, HD), 0:nk], probs))
-            act[toks, FF:ACT] = jnp.concatenate(ctx, axis=0).T.astype(BF16)
-
-        for off in (2, 3, 1, 0):
-            zz = lax.rem(z + off, R)
-            rows = pl.ds(pl.multiple_of(zz * GROUP, GROUP), GROUP)
-            part[zz] = nn_dot(act[rows, :], wcat[...]).astype(BF16).reshape(R, BLK, D)
-            k1 = (R - off) % R
-            q1(c, 1, k1).start()
-            if off == 2:
+        with jax.named_scope("wait_g0"):
+            others(1, 0, (0,))
+            others(1, 1, (0,))
+            p3(c, 1, 0, True).wait_recv()
+        with jax.named_scope("norm0"):
+            norms(c, 0, 0)
+        with jax.named_scope("wait_g3"):
+            for k in ORDER[1:]:
+                forward(k)
+            others(0, 0, (0, 1, 2))
+            others(1, 0, (1,))
+            p3(c, 1, 1, True).wait_recv()
+
+        @pl.when((c < CHUNKS - 1) & (lax.rem(stage, 2) == 1))
+        def _():
+            pl.semaphore_signal(turn_sem, inc=1, device_id={"pp": stage - 1}, device_id_type=MESH)
+
+        with jax.named_scope("norm3"):
+            norms(c, 3, 1)
+
+        @pl.when(c == 0)
+        def _():
+            for cp in weight_copies:
+                cp.wait()
+
+        with jax.named_scope("proj03"):
+            project((0, 3))
+        with jax.named_scope("wait_g1"):
+            others(0, 1, (0, 3))
+            others(1, 1, (3,))
+            p3(c, 1, 3, True).wait_recv()
+        with jax.named_scope("norm1"):
+            norms(c, 1, 0)
+        with jax.named_scope("wait_g2"):
+            for k in ORDER:
+                p3(c, 0, k, True).wait_recv()
+            others(1, 0, (2,))
+            p3(c, 1, 2, True).wait_recv()
+        with jax.named_scope("norm2"):
+            norms(c, 2, 1)
+        with jax.named_scope("proj12"):
+            project((1, 2))
+
+        with jax.named_scope("attn"):
+            for qb in range(2):
+                toks = pl.ds(qb * 256, 256)
+                nk = (qb + 1) * 256
+                ctx = []
+                for hd in range(HEADS):
+                    scores = nn_dot(ks[hd, 0:nk, :], qv[pl.ds(hd * HD, HD), toks]) * (HD ** -0.5)
+                    key_pos = lax.broadcasted_iota(jnp.int32, (nk, 256), 0)
+                    query_pos = lax.broadcasted_iota(jnp.int32, (nk, 256), 1) + qb * 256
+                    scores = jnp.where(query_pos >= key_pos, scores, -1e30)
+                    top = jnp.max(scores, axis=0, keepdims=True)
+                    probs = jnp.exp(scores - top)
+                    total = jnp.sum(probs, axis=0, keepdims=True)
+                    probs = (probs * (1.0 / total)).astype(BF16)
+                    ctx.append(nn_dot(qv[pl.ds(nqk + hd * HD, HD), 0:nk], probs))
+                act[toks, FF:ACT] = jnp.concatenate(ctx, axis=0).T.astype(BF16)
+
+        with jax.named_scope("down"):
+            for off in (2, 3, 1, 0):
+                zz = lax.rem(z + off, R)
+                rows = pl.ds(pl.multiple_of(zz * GROUP, GROUP), GROUP)
+                part[zz] = nn_dot(act[rows, :], wcat[...]).astype(BF16).reshape(R, BLK, D)
+                k1 = (R - off) % R
+                q1(c, 1, k1).start()
                 for k in ORDER:
-                    q1(c, 0, k).start()
-            elif off == 3:
-                for k in ORDER:
-                    if SIDE[k] == 0:
+                    if off == 2:
+                        q1(c, 0, k).start()
+                    elif off == 3 and (k == 0 or SIDE[k] == 0):
                         q2(c, 0, 1, k).start()
-            elif off == 1:
-                for k in ORDER:
-                    if SIDE[k] == 1:
+                    elif off == 1 and (k == 0 or SIDE[k] == 1):
                         q2(c, 0, 0, k).start()
-            q2(c, 1, 1 - SIDE[k1], k1).start()
-
-        for h, k in [(0, 0), (0, 1), (1, 2), (0, 3), (0, 2), (1, 1), (1, 3), (1, 0)]:
-            side = SIDE[k]
-            q1(c, h, k).wait_recv()
-            mine = partial_at(h, (1, -1)[side], -k)
-            mine[...] = (mine[...].astype(F32) + r1[c, h, k].astype(F32)).astype(BF16)
-            q2(c, h, side, k).start()
-        for k in (1, 2, 3, 0):
-            for h in range(2):
+                for side in range(2):
+                    if k1 == 0 or SIDE[k1] != side:
+                        q2(c, 1, side, k1).start()
+
+        with jax.named_scope("rs_add"):
+            for h, k in [(0, 1), (0, 3), (0, 2), (1, 2), (1, 1), (1, 3)]:
+                side = SIDE[k]
+                q1(c, h, k).wait_recv()
+                mine = partial_at(h, (1, -1)[side], -k)
+                mine[...] = (mine[...].astype(F32) + r1[c, h, k].astype(F32)).astype(BF16)
+                q2(c, h, side, k).start()
+        with jax.named_scope("rs_mid"):
+            for h, k in [(0, 1), (0, 3), (0, 2), (1, 2), (1, 1), (1, 3), (0, 0), (1, 0)]:
                 q2(c, h, 0, k).wait_recv()
                 q2(c, h, 1, k).wait_recv()
                 total = partial_at(h, 0, -k)[...].astype(F32) + r2[c, h, k].astype(F32) + r3[c, h, k].astype(F32)
+                if k == 0:
+                    q1(c, h, 0).wait_recv()
+                    total += r1[c, h, 0].astype(F32)
                 mid[h, k] = total.astype(BF16)
                 if k:
                     q3(c, h, k).start()
-        for h in range(2):
-            rows = pl.ds(h * SUB, SUB)
-            total = xg[c, z, y, rows, :].astype(F32) + mid[h, 0].astype(F32)
-            for k in (1, 2, 3):
-                q3(c, h, k).wait_recv()
-                total += r4[c, h, k - 1].astype(F32)
-            ybuf[c, rows, :] = total.astype(BF16)
+        with jax.named_scope("rs_fin"):
+            for h in range(2):
+                rows = pl.ds(h * SUB, SUB)
+                total = xg[c, z, y, rows, :].astype(F32) + mid[h, 0].astype(F32)
+                for k in (1, 2, 3):
+                    q3(c, h, k).wait_recv()
+                    total += r4[c, h, k - 1].astype(F32)
+                ybuf[c, rows, :] = total.astype(BF16)
 
         @pl.when(stage < last)
         def _():
@@ -342,8 +371,8 @@
                 pltpu.VMEM((QKV, D), BF16),
                 pltpu.VMEM((D, FF), BF16),
                 pltpu.VMEM((ACT, D), BF16),
-                pltpu.VMEM((GROUP, D), BF16),
-                pltpu.VMEM((GROUP, D), BF16),
+                pltpu.VMEM((2 * GROUP, D), BF16),
+                pltpu.VMEM((2 * GROUP, D), BF16),
                 pltpu.VMEM((2 * flat, SEQ), BF16),
                 pltpu.VMEM((HEADS, SEQ, HD), BF16),
                 pltpu.VMEM((SEQ, ACT), BF16),
@@ -357,6 +386,7 @@
                 dma((6,)), dma((CHUNKS,)), dma((CHUNKS,)), dma((CHUNKS,)), dma((CHUNKS,)),
                 dma((2, 3)), dma((CHUNKS, 2, 3)), dma((2, 2, R)), dma((CHUNKS, 2, 2, R)), dma((2, R)), dma((CHUNKS, 2, R)),
                 dma((2, R)), dma((CHUNKS, 2, R)), dma((2, 2, R)), dma((CHUNKS, 2, 2, R)), dma((2, 3)), dma((CHUNKS, 2, 3)),
+                pltpu.SemaphoreType.REGULAR,
             ],
             compiler_params=pltpu.CompilerParams(collective_id=1, has_side_effects=True, vmem_limit_bytes=62 * 2**20),
             name="pipeline",

time: 535 us -> 435 us (0.81)
  Pallas kernels: 533 us -> 433 us
    pallas_call x1, Pallas kernels: 533 us -> 433 us  [body(): pl.pallas_call(functools.partial(kernel, pp_size), out_shape=jax.ShapeDty...]
where the time goes in v3:
time: 435 us
  Pallas kernels  433 us (100%)
    pallas_call x1, Pallas kernels, body(): pl.pallas_call(functools.partial(kernel, pp_size), out_shape=jax.ShapeDty...  433 us

profile of v3, /device:TPU:7, one launch (start us, length us, event | category | flops | bytes accessed | tf_op | source)
XLA Modules:
  0.0 434.9 jit_solution(14537986505250222380)
XLA Ops:
  0.0 432.9 %pipeline.1 = bf16[2,2,32,2560]{3,2,1,0:T(8,128)(2,1)} custom-call(bf16[2,2,32,2560]{3,2,1,0:T(8,128)(2,1)} %x_ref.1, f32[4,2560]{1,0:T(4,128)} %bitcast.27, bf16[160,2560]{1,0:T(8,128)(2,1)} %bitcast.23, bf16[160,2560]{1,0:T(8,128)(2,1)} %bitcast.24, bf16[160,2560]{1,0:T(8,128)(2,1)} %bitcast.25, bf16[160,2560]{1,0:T(8,128)(2,1)} %bitcast.26, ...), custom_call_target="tpu_custom_call" | custom-call | tf_op jit(solution)/shard_map/pipeline/pallas_call | solution.py:364
  432.9 2.0 copy.12

commit v4 on v3

--- a/solution.py
+++ b/solution.py
@@ -48,11 +48,13 @@
 def kernel(pp_size, x_ref, ln_ref, wq_ref, wk_ref, wv_ref, wo_ref, wup_ref, wdown_ref, cos_ref, sin_ref, out_ref,
            xg, wqkv, wup, wcat, ha, hm, qv, ks, act, part, r1, r2, r3, mid, r4, ybuf,
            w_sem, in_sem, out_sem, hop_send, hop_recv, p1_send, p1_recv, p2_send, p2_recv, p3_send, p3_recv,
-           q1_send, q1_recv, q2_send, q2_recv, q3_send, q3_recv, turn_sem):
+           q1_send, q1_recv, q2_send, q2_recv, q3_send, q3_recv, direct_send, turn_sem):
     tp = lax.axis_index("tp")
     stage = lax.axis_index("pp")
     z, y = lax.div(tp, R), lax.rem(tp, R)
     last = pp_size - 1
+    even = lax.rem(stage, 2) == 0
+    partner = stage + 1 - 2 * lax.rem(stage, 2)
     nqk = HEADS * HD
 
     home = ((z, y), (y, z))
@@ -60,10 +62,10 @@
     def at(h, v, u):
         return (v, u) if h == 0 else (u, v)
 
-    def peer(h, dv, du):
+    def peer(h, dv, du, pp=stage):
         v, u = home[h]
         zz, yy = at(h, lax.rem(v + dv, R), lax.rem(u + du, R))
-        return {"tp": zz * R + yy}
+        return {"tp": zz * R + yy, "pp": pp}
 
     def remote(src, dst, send, recv, device):
         return pltpu.make_async_remote_copy(src_ref=src, dst_ref=dst, send_sem=send, recv_sem=recv, device_id=device, device_id_type=MESH)
@@ -72,6 +74,7 @@
     for d in (1, 2, 3):
         for h in range(2):
             pl.semaphore_signal(barrier, inc=1, device_id=peer(h, 0, d), device_id_type=MESH)
+            pl.semaphore_signal(barrier, inc=1, device_id=peer(h, 0, d, partner), device_id_type=MESH)
 
     @pl.when(stage > 0)
     def _():
@@ -101,7 +104,7 @@
     for cp in weight_copies:
         cp.start()
 
-    pl.semaphore_wait(barrier, 6 + jnp.where(stage > 0, 1, 0) + jnp.where(stage < last, 1, 0))
+    pl.semaphore_wait(barrier, 12 + jnp.where(stage > 0, 1, 0) + jnp.where(stage < last, 1, 0))
 
     def hop_copy(c):
         return remote(ybuf.at[c], xg.at[c, z, y], hop_send.at[c], hop_recv.at[c], {"pp": lax.rem(stage + 1, pp_size)})
@@ -144,23 +147,40 @@
     def q3(c, h, k):
         return remote(mid.at[h, k], r4.at[c, h, k - 1], q3_send.at[h, k - 1], q3_recv.at[c, h, k - 1], peer(h, 0, R - k))
 
-    def norms(c, off, slot):
-        zz = lax.rem(z + off, R)
-        for yy in range(R):
-            total = jnp.sum(xg[c, zz, yy].astype(F32), axis=-1, keepdims=True)
+    def first_sends(c, direct=False):
+        src_dev = stage + 1 if direct else stage
+        copies = []
+        for h in range(2):
+            for i, (hh, dv, du) in enumerate([(h, 0, 1), (h, 0, 3), (1 - h, 1, 0), (1 - h, 3, 0), (h, 0, 2), (1 - h, 2, 0)]):
+                dst = gathered(c, hh, 0, 0)
+                src = ybuf.at[c, pl.ds(hh * SUB, SUB), :] if direct else dst
+                if du:
+                    send, recv = p1_send.at[hh, du - 1], p1_recv.at[c, hh, du - 1]
+                elif dv == 2:
+                    send, recv = p3_send.at[hh, 0], p3_recv.at[c, hh, 0]
+                else:
+                    send, recv = p2_send.at[hh, dv // 2, 0], p2_recv.at[c, hh, dv // 2, 0]
+                copies.append(remote(src, dst, direct_send.at[c, h, i] if direct else send, recv, peer(hh, dv, du, src_dev)))
+        return copies
+
+    def norms(c, blocks):
+        for h, dv, du in blocks:
+            block = gathered(c, h, dv, du)
+            zz, yy = place(h, dv, du)
+            total = jnp.sum(block[...].astype(F32), axis=-1, keepdims=True)
             mean = total * (1.0 / D)
-            dev = xg[c, zz, yy].astype(F32) - mean
+            dev = block[...].astype(F32) - mean
             var = jnp.sum(dev * dev, axis=-1, keepdims=True) * (1.0 / D)
             scale = lax.rsqrt(var + LN_EPS)
-            unit = (xg[c, zz, yy].astype(F32) - mean) * scale
-            dst = pl.ds(slot * GROUP + yy * BLK, BLK)
+            unit = (block[...].astype(F32) - mean) * scale
+            dst = pl.ds(pl.multiple_of(zz * GROUP + yy * BLK + h * SUB, SUB), SUB)
             ha[dst, :] = (unit * ln_ref[0:1, :] + ln_ref[1:2, :]).astype(BF16)
             hm[dst, :] = (unit * ln_ref[2:3, :] + ln_ref[3:4, :]).astype(BF16)
 
     def project(offs):
         toks = [pl.ds(pl.multiple_of(lax.rem(z + off, R) * GROUP, GROUP), GROUP) for off in offs]
 
-        proj = nt_dot(wqkv[...], ha[...])
+        proj = nt_dot(wqkv[...], jnp.concatenate([ha[tok, :] for tok in toks], axis=0))
         for slot, tok in enumerate(toks):
             cols = proj[:, slot * GROUP:(slot + 1) * GROUP]
             cos, sin = cos_ref[:, tok], sin_ref[:, tok]
@@ -174,8 +194,8 @@
                 ks[hd, tok, :] = rope(nqk + hd * HD).T.astype(BF16)
             qv[pl.ds(nqk, nqk), tok] = cols[2 * nqk:].astype(BF16)
 
-        for slot, tok in enumerate(toks):
-            pre = nn_dot(hm[slot * GROUP:(slot + 1) * GROUP, :], wup[...])
+        for tok in toks:
+            pre = nn_dot(hm[tok, :], wup[...])
             act[tok, 0:FF] = (0.5 * pre * (1.0 + lax.erf(pre * np.float32(0.5 ** 0.5)))).astype(BF16)
 
     def chunk(c, carry):
@@ -188,75 +208,71 @@
             def _():
                 hop_copy(c).wait_recv()
 
-            @pl.when((c > 0) & (lax.rem(stage, 2) == 0))
+            @pl.when((c > 0) & even)
             def _():
                 pl.semaphore_wait(turn_sem, 1)
 
+            @pl.when(even)
+            def _():
+                for cp in first_sends(c):
+                    cp.start()
+
         with jax.named_scope("p1_wait"):
-            for h in range(2):
-                for d in (1, 3):
-                    p1(c, h, d).start()
-                for side in range(2):
-                    p2(c, 1 - h, side, 0).start()
-                p1(c, h, 2).start()
-                p3(c, 1 - h, 0).start()
             for k in ORDER[1:]:
                 for h in range(2):
                     p1(c, h, k, True).wait_recv()
                     for side in range(2):
                         p2(c, h, side, k).start()
-
-        def forward(k):
+        with jax.named_scope("norm_a"):
+            norms(c, [(h, 0, -k) for k in ORDER for h in range(2)])
+        with jax.named_scope("wait_b"):
+            for h in (1, 0):
+                for side in range(2):
+                    p2(c, h, side, 0, True).wait_recv()
+                p3(c, h, 0, True).wait_recv()
+        with jax.named_scope("norm_b"):
+            norms(c, [(h, dv, 0) for h in (1, 0) for dv in (-1, 1, 2)])
+        def rest(k):
             for h in range(2):
-                p2(c, h, SIDE[k], k, True).wait_recv()
-                p3(c, h, k).start()
-
-        def others(h, side, ks_):
-            for k in ks_:
-                p2(c, h, side, k, True).wait_recv()
-
-        with jax.named_scope("wait_g0"):
-            others(1, 0, (0,))
-            others(1, 1, (0,))
-            p3(c, 1, 0, True).wait_recv()
-        with jax.named_scope("norm0"):
-            norms(c, 0, 0)
-        with jax.named_scope("wait_g3"):
+                p2(c, h, 1 - SIDE[k], k, True).wait_recv()
+            norms(c, [(h, dv, -k) for h in range(2) for dv in (-1, 1)])
+
+        with jax.named_scope("forward"):
             for k in ORDER[1:]:
-                forward(k)
-            others(0, 0, (0, 1, 2))
-            others(1, 0, (1,))
-            p3(c, 1, 1, True).wait_recv()
-
-        @pl.when((c < CHUNKS - 1) & (lax.rem(stage, 2) == 1))
+                for h in range(2):
+                    p2(c, h, SIDE[k], k, True).wait_recv()
+                    p3(c, h, k).start()
+                if k != ORDER[-1]:
+                    rest(k)
+
+        @pl.when((c < CHUNKS - 1) & jnp.logical_not(even))
         def _():
             pl.semaphore_signal(turn_sem, inc=1, device_id={"pp": stage - 1}, device_id_type=MESH)
-
-        with jax.named_scope("norm3"):
-            norms(c, 3, 1)
 
         @pl.when(c == 0)
         def _():
             for cp in weight_copies:
                 cp.wait()
 
-        with jax.named_scope("proj03"):
-            project((0, 3))
-        with jax.named_scope("wait_g1"):
-            others(0, 1, (0, 3))
-            others(1, 1, (3,))
-            p3(c, 1, 3, True).wait_recv()
-        with jax.named_scope("norm1"):
-            norms(c, 1, 0)
-        with jax.named_scope("wait_g2"):
-            for k in ORDER:
+        with jax.named_scope("proj0"):
+            project((0,))
+        with jax.named_scope("norm_c"):
+            rest(ORDER[-1])
+        with jax.named_scope("wait_e"):
+            for k in (1, 3):
+                p3(c, 1, k, True).wait_recv()
+        with jax.named_scope("norm_e"):
+            norms(c, [(1, 2, -1), (1, 2, -3)])
+        with jax.named_scope("proj31"):
+            project((3, 1))
+        with jax.named_scope("wait_f"):
+            p3(c, 1, 2, True).wait_recv()
+            for k in ORDER[1:]:
                 p3(c, 0, k, True).wait_recv()
-            others(1, 0, (2,))
-            p3(c, 1, 2, True).wait_recv()
-        with jax.named_scope("norm2"):
-            norms(c, 2, 1)
-        with jax.named_scope("proj12"):
-            project((1, 2))
+        with jax.named_scope("norm_f"):
+            norms(c, [(1, 2, -2)] + [(0, 2, -k) for k in ORDER[1:]])
+        with jax.named_scope("proj2"):
+            project((2,))
 
         with jax.named_scope("attn"):
             for qb in range(2):
@@ -275,33 +291,37 @@
                     ctx.append(nn_dot(qv[pl.ds(nqk + hd * HD, HD), 0:nk], probs))
                 act[toks, FF:ACT] = jnp.concatenate(ctx, axis=0).T.astype(BF16)
 
+        def down(blocks):
+            rows = []
+            for h, dv, du in blocks:
+                zz, yy = place(h, dv, du)
+                rows.append(act[pl.ds(pl.multiple_of(zz * GROUP + yy * BLK + h * SUB, SUB), SUB), :])
+            out = nn_dot(jnp.concatenate(rows, axis=0), wcat[...]).astype(BF16)
+            for i, (h, dv, du) in enumerate(blocks):
+                partial_at(h, dv, du)[...] = out[i * SUB:(i + 1) * SUB]
+
         with jax.named_scope("down"):
-            for off in (2, 3, 1, 0):
-                zz = lax.rem(z + off, R)
-                rows = pl.ds(pl.multiple_of(zz * GROUP, GROUP), GROUP)
-                part[zz] = nn_dot(act[rows, :], wcat[...]).astype(BF16).reshape(R, BLK, D)
-                k1 = (R - off) % R
-                q1(c, 1, k1).start()
+            down([(h, 2, -k) for h in range(2) for k in ORDER])
+            for k in (1, 3, 2, 0):
+                for h in range(2):
+                    q1(c, h, k).start()
+            for h in range(2):
+                down([(h, dv, -k) for dv in (1, -1) for k in ORDER])
                 for k in ORDER:
-                    if off == 2:
-                        q1(c, 0, k).start()
-                    elif off == 3 and (k == 0 or SIDE[k] == 0):
-                        q2(c, 0, 1, k).start()
-                    elif off == 1 and (k == 0 or SIDE[k] == 1):
-                        q2(c, 0, 0, k).start()
-                for side in range(2):
-                    if k1 == 0 or SIDE[k1] != side:
-                        q2(c, 1, side, k1).start()
+                    for side in range(2):
+                        if k == 0 or SIDE[k] != side:
+                            q2(c, h, side, k).start()
+            down([(h, 0, -k) for h in range(2) for k in ORDER])
 
         with jax.named_scope("rs_add"):
-            for h, k in [(0, 1), (0, 3), (0, 2), (1, 2), (1, 1), (1, 3)]:
+            for h, k in [(0, 1), (1, 1), (0, 3), (1, 3), (0, 2), (1, 2)]:
                 side = SIDE[k]
                 q1(c, h, k).wait_recv()
                 mine = partial_at(h, (1, -1)[side], -k)
                 mine[...] = (mine[...].astype(F32) + r1[c, h, k].astype(F32)).astype(BF16)
                 q2(c, h, side, k).start()
         with jax.named_scope("rs_mid"):
-            for h, k in [(0, 1), (0, 3), (0, 2), (1, 2), (1, 1), (1, 3), (0, 0), (1, 0)]:
+            for h, k in [(0, 1), (1, 1), (0, 3), (1, 3), (0, 2), (1, 2), (0, 0), (1, 0)]:
                 q2(c, h, 0, k).wait_recv()
                 q2(c, h, 1, k).wait_recv()
                 total = partial_at(h, 0, -k)[...].astype(F32) + r2[c, h, k].astype(F32) + r3[c, h, k].astype(F32)
@@ -324,17 +344,27 @@
         def _():
             hop_copy(c).start()
 
+        @pl.when(even)
+        def _():
+            for cp in first_sends(c, True):
+                cp.start()
+
         out_copy(c).start()
+
+        @pl.when(even)
+        def _():
+            for cp in first_sends(c):
+                cp.wait_send()
 
         for h in range(2):
             for k in range(R):
                 if k:
-                    p1(c, h, k).wait_send()
                     q3(c, h, k).wait_send()
+                    p3(c, h, k).wait_send()
                 for side in range(2):
-                    p2(c, h, side, k).wait_send()
+                    if k:
+                        p2(c, h, side, k).wait_send()
                     q2(c, h, side, k).wait_send()
-                p3(c, h, k).wait_send()
                 q1(c, h, k).wait_send()
         return carry
 
@@ -346,6 +376,11 @@
         @pl.when(stage < last)
         def _():
             hop_copy(c).wait_send()
+
+        @pl.when(even)
+        def _():
+            for cp in first_sends(c, True):
+                cp.wait_send()
 
 
 def solution(mesh):
@@ -371,8 +406,8 @@
                 pltpu.VMEM((QKV, D), BF16),
                 pltpu.VMEM((D, FF), BF16),
                 pltpu.VMEM((ACT, D), BF16),
-                pltpu.VMEM((2 * GROUP, D), BF16),
-                pltpu.VMEM((2 * GROUP, D), BF16),
+                pltpu.VMEM((SEQ, D), BF16),
+                pltpu.VMEM((SEQ, D), BF16),
                 pltpu.VMEM((2 * flat, SEQ), BF16),
                 pltpu.VMEM((HEADS, SEQ, HD), BF16),
                 pltpu.VMEM((SEQ, ACT), BF16),
@@ -386,7 +421,7 @@
                 dma((6,)), dma((CHUNKS,)), dma((CHUNKS,)), dma((CHUNKS,)), dma((CHUNKS,)),
                 dma((2, 3)), dma((CHUNKS, 2, 3)), dma((2, 2, R)), dma((CHUNKS, 2, 2, R)), dma((2, R)), dma((CHUNKS, 2, R)),
                 dma((2, R)), dma((CHUNKS, 2, R)), dma((2, 2, R)), dma((CHUNKS, 2, 2, R)), dma((2, 3)), dma((CHUNKS, 2, 3)),
-                pltpu.SemaphoreType.REGULAR,
+                dma((CHUNKS, 2, 6)), pltpu.SemaphoreType.REGULAR,
             ],
             compiler_params=pltpu.CompilerParams(collective_id=1, has_side_effects=True, vmem_limit_bytes=62 * 2**20),
             name="pipeline",

time: 435 us -> 423 us (0.972)
  Pallas kernels: 433 us -> 421 us
    pallas_call x1, Pallas kernels: 433 us -> 421 us  [body(): pl.pallas_call(functools.partial(kernel, pp_size), out_shape=jax.ShapeDty...]
where the time goes in v4:
time: 423 us
  Pallas kernels  421 us (100%)
    pallas_call x1, Pallas kernels, body(): pl.pallas_call(functools.partial(kernel, pp_size), out_shape=jax.ShapeDty...  421 us

profile of v4, /device:TPU:7, one launch (start us, length us, event | category | flops | bytes accessed | tf_op | source)
XLA Modules:
  0.0 422.7 jit_solution(14372562841806480275)
XLA Ops:
  0.0 420.7 %pipeline.1 = bf16[2,2,32,2560]{3,2,1,0:T(8,128)(2,1)} custom-call(bf16[2,2,32,2560]{3,2,1,0:T(8,128)(2,1)} %x_ref.1, f32[4,2560]{1,0:T(4,128)} %bitcast.27, bf16[160,2560]{1,0:T(8,128)(2,1)} %bitcast.23, bf16[160,2560]{1,0:T(8,128)(2,1)} %bitcast.24, bf16[160,2560]{1,0:T(8,128)(2,1)} %bitcast.25, bf16[160,2560]{1,0:T(8,128)(2,1)} %bitcast.26, ...), custom_call_target="tpu_custom_call" | custom-call | tf_op jit(solution)/shard_map/pipeline/pallas_call | solution.py:399
  420.7 2.0 copy.12

commit v5 on v4

--- a/solution.py
+++ b/solution.py
@@ -20,6 +20,7 @@
 SUB = BLK // 2
 GROUP = R * BLK
 ORDER = (0, 1, 3, 2)
+LATE = ((0, 1), (0, 3), (1, 3), (0, 2), (1, 2))
 SIDE = (0, 1, 1, 0)
 HEADS = 2
 HD = 80
@@ -138,7 +139,7 @@
         return remote(view, view, p3_send.at[h, k], p3_recv.at[c, h, k], peer(h, (1, R - 1)[side] if k else 2, 0))
 
     def q1(c, h, k):
-        return remote(partial_at(h, 2, -k), r1.at[c, h, k], q1_send.at[h, k], q1_recv.at[c, h, k], peer(h, (1, R - 1)[SIDE[k]] if k else 2, 0))
+        return remote(partial_at(h, 2, -k), r1.at[c, h, k], q1_send.at[h, k], q1_recv.at[c, h, k], peer(h, (1, R - 1)[SIDE[k]], 0))
 
     def q2(c, h, side, k):
         return remote(partial_at(h, (1, -1)[side], -k), (r2 if side == 0 else r3).at[c, h, k], q2_send.at[h, side, k], q2_recv.at[c, h, side, k],
@@ -254,25 +255,21 @@
             for cp in weight_copies:
                 cp.wait()
 
-        with jax.named_scope("proj0"):
-            project((0,))
         with jax.named_scope("norm_c"):
             rest(ORDER[-1])
         with jax.named_scope("wait_e"):
-            for k in (1, 3):
-                p3(c, 1, k, True).wait_recv()
+            p3(c, 1, 1, True).wait_recv()
         with jax.named_scope("norm_e"):
-            norms(c, [(1, 2, -1), (1, 2, -3)])
-        with jax.named_scope("proj31"):
-            project((3, 1))
+            norms(c, [(1, 2, -1)])
+        with jax.named_scope("proj03"):
+            project((0, 3))
         with jax.named_scope("wait_f"):
-            p3(c, 1, 2, True).wait_recv()
-            for k in ORDER[1:]:
-                p3(c, 0, k, True).wait_recv()
+            for h, k in LATE:
+                p3(c, h, k, True).wait_recv()
         with jax.named_scope("norm_f"):
-            norms(c, [(1, 2, -2)] + [(0, 2, -k) for k in ORDER[1:]])
-        with jax.named_scope("proj2"):
-            project((2,))
+            norms(c, [(h, 2, -k) for h, k in LATE])
+        with jax.named_scope("proj12"):
+            project((1, 2))
 
         with jax.named_scope("attn"):
             for qb in range(2):
@@ -309,12 +306,12 @@
                 down([(h, dv, -k) for dv in (1, -1) for k in ORDER])
                 for k in ORDER:
                     for side in range(2):
-                        if k == 0 or SIDE[k] != side:
+                        if SIDE[k] != side:
                             q2(c, h, side, k).start()
             down([(h, 0, -k) for h in range(2) for k in ORDER])
 
         with jax.named_scope("rs_add"):
-            for h, k in [(0, 1), (1, 1), (0, 3), (1, 3), (0, 2), (1, 2)]:
+            for h, k in [(0, 1), (1, 1), (0, 3), (1, 3), (0, 2), (1, 2), (0, 0), (1, 0)]:
                 side = SIDE[k]
                 q1(c, h, k).wait_recv()
                 mine = partial_at(h, (1, -1)[side], -k)
@@ -325,9 +322,6 @@
                 q2(c, h, 0, k).wait_recv()
                 q2(c, h, 1, k).wait_recv()
                 total = partial_at(h, 0, -k)[...].astype(F32) + r2[c, h, k].astype(F32) + r3[c, h, k].astype(F32)
-                if k == 0:
-                    q1(c, h, 0).wait_recv()
-                    total += r1[c, h, 0].astype(F32)
                 mid[h, k] = total.astype(BF16)
                 if k:
                     q3(c, h, k).start()

time: 423 us -> 407 us (0.962)
  Pallas kernels: 421 us -> 405 us
    pallas_call x1, Pallas kernels: 421 us -> 405 us  [body(): pl.pallas_call(functools.partial(kernel, pp_size), out_shape=jax.ShapeDty...]
where the time goes in v5:
time: 407 us
  Pallas kernels  405 us (100%)
    pallas_call x1, Pallas kernels, body(): pl.pallas_call(functools.partial(kernel, pp_size), out_shape=jax.ShapeDty...  405 us

profile of v5, /device:TPU:7, one launch (start us, length us, event | category | flops | bytes accessed | tf_op | source)
XLA Modules:
  0.0 407.2 jit_solution(15393788490718443443)
XLA Ops:
  0.0 405.2 %pipeline.1 = bf16[2,2,32,2560]{3,2,1,0:T(8,128)(2,1)} custom-call(bf16[2,2,32,2560]{3,2,1,0:T(8,128)(2,1)} %x_ref.1, f32[4,2560]{1,0:T(4,128)} %bitcast.27, bf16[160,2560]{1,0:T(8,128)(2,1)} %bitcast.23, bf16[160,2560]{1,0:T(8,128)(2,1)} %bitcast.24, bf16[160,2560]{1,0:T(8,128)(2,1)} %bitcast.25, bf16[160,2560]{1,0:T(8,128)(2,1)} %bitcast.26, ...), custom_call_target="tpu_custom_call" | custom-call | tf_op jit(solution)/shard_map/pipeline/pallas_call | solution.py:393
  405.2 2.0 copy.12

commit v6 on v5

--- a/solution.py
+++ b/solution.py
@@ -20,6 +20,7 @@
 SUB = BLK // 2
 GROUP = R * BLK
 ORDER = (0, 1, 3, 2)
+BACK = (2, 1, 3, 0)
 LATE = ((0, 1), (0, 3), (1, 3), (0, 2), (1, 2))
 SIDE = (0, 1, 1, 0)
 HEADS = 2
@@ -299,26 +300,26 @@
 
         with jax.named_scope("down"):
             down([(h, 2, -k) for h in range(2) for k in ORDER])
-            for k in (1, 3, 2, 0):
+            for k in BACK:
                 for h in range(2):
                     q1(c, h, k).start()
             for h in range(2):
                 down([(h, dv, -k) for dv in (1, -1) for k in ORDER])
-                for k in ORDER:
+                for k in BACK:
                     for side in range(2):
                         if SIDE[k] != side:
                             q2(c, h, side, k).start()
             down([(h, 0, -k) for h in range(2) for k in ORDER])
 
         with jax.named_scope("rs_add"):
-            for h, k in [(0, 1), (1, 1), (0, 3), (1, 3), (0, 2), (1, 2), (0, 0), (1, 0)]:
+            for h, k in [(h, k) for k in BACK for h in range(2)]:
                 side = SIDE[k]
                 q1(c, h, k).wait_recv()
                 mine = partial_at(h, (1, -1)[side], -k)
                 mine[...] = (mine[...].astype(F32) + r1[c, h, k].astype(F32)).astype(BF16)
                 q2(c, h, side, k).start()
         with jax.named_scope("rs_mid"):
-            for h, k in [(0, 1), (1, 1), (0, 3), (1, 3), (0, 2), (1, 2), (0, 0), (1, 0)]:
+            for h, k in [(h, k) for k in BACK for h in range(2)]:
                 q2(c, h, 0, k).wait_recv()
                 q2(c, h, 1, k).wait_recv()
                 total = partial_at(h, 0, -k)[...].astype(F32) + r2[c, h, k].astype(F32) + r3[c, h, k].astype(F32)

time: 407 us -> 400 us (0.983)
  Pallas kernels: 405 us -> 398 us
    pallas_call x1, Pallas kernels: 405 us -> 398 us  [body(): pl.pallas_call(functools.partial(kernel, pp_size), out_shape=jax.ShapeDty...]
where the time goes in v6:
time: 400 us
  Pallas kernels  398 us (100%)
    pallas_call x1, Pallas kernels, body(): pl.pallas_call(functools.partial(kernel, pp_size), out_shape=jax.ShapeDty...  398 us

profile of v6, /device:TPU:7, one launch (start us, length us, event | category | flops | bytes accessed | tf_op | source)
XLA Modules:
  0.0 399.7 jit_solution(13369008149466661608)
XLA Ops:
  0.0 397.7 %pipeline.1 = bf16[2,2,32,2560]{3,2,1,0:T(8,128)(2,1)} custom-call(bf16[2,2,32,2560]{3,2,1,0:T(8,128)(2,1)} %x_ref.1, f32[4,2560]{1,0:T(4,128)} %bitcast.27, bf16[160,2560]{1,0:T(8,128)(2,1)} %bitcast.23, bf16[160,2560]{1,0:T(8,128)(2,1)} %bitcast.24, bf16[160,2560]{1,0:T(8,128)(2,1)} %bitcast.25, bf16[160,2560]{1,0:T(8,128)(2,1)} %bitcast.26, ...), custom_call_target="tpu_custom_call" | custom-call | tf_op jit(solution)/shard_map/pipeline/pallas_call | solution.py:394
  397.7 2.0 copy.12

commit v7 on v6

--- a/solution.py
+++ b/solution.py
@@ -276,17 +276,14 @@
             for qb in range(2):
                 toks = pl.ds(qb * 256, 256)
                 nk = (qb + 1) * 256
-                ctx = []
-                for hd in range(HEADS):
-                    scores = nn_dot(ks[hd, 0:nk, :], qv[pl.ds(hd * HD, HD), toks]) * (HD ** -0.5)
-                    key_pos = lax.broadcasted_iota(jnp.int32, (nk, 256), 0)
-                    query_pos = lax.broadcasted_iota(jnp.int32, (nk, 256), 1) + qb * 256
-                    scores = jnp.where(query_pos >= key_pos, scores, -1e30)
-                    top = jnp.max(scores, axis=0, keepdims=True)
-                    probs = jnp.exp(scores - top)
-                    total = jnp.sum(probs, axis=0, keepdims=True)
-                    probs = (probs * (1.0 / total)).astype(BF16)
-                    ctx.append(nn_dot(qv[pl.ds(nqk + hd * HD, HD), 0:nk], probs))
+                key_pos = lax.broadcasted_iota(jnp.int32, (nk, 256), 0)
+                query_pos = lax.broadcasted_iota(jnp.int32, (nk, 256), 1) + qb * 256
+                allowed = query_pos >= key_pos
+                scores = [nn_dot(ks[hd, 0:nk, :], qv[pl.ds(hd * HD, HD), toks]) * (HD ** -0.5) for hd in range(HEADS)]
+                scores = [jnp.where(allowed, sc, -1e30) for sc in scores]
+                probs = [jnp.exp(sc - jnp.max(sc, axis=0, keepdims=True)) for sc in scores]
+                probs = [(pr * (1.0 / jnp.sum(pr, axis=0, keepdims=True))).astype(BF16) for pr in probs]
+                ctx = [nn_dot(qv[pl.ds(nqk + hd * HD, HD), 0:nk], probs[hd]) for hd in range(HEADS)]
                 act[toks, FF:ACT] = jnp.concatenate(ctx, axis=0).T.astype(BF16)
 
         def down(blocks):

time: 400 us -> 398 us (level)
  no operation moved by 1% of the time
where the time goes in v7:
time: 398 us
  Pallas kernels  396 us (99%)
    pallas_call x1, Pallas kernels, body(): pl.pallas_call(functools.partial(kernel, pp_size), out_shape=jax.ShapeDty...  396 us

profile of v7, /device:TPU:7, one launch (start us, length us, event | category | flops | bytes accessed | tf_op | source)
XLA Modules:
  0.0 397.8 jit_solution(16466686264975026675)
XLA Ops:
  0.0 395.8 %pipeline.1 = bf16[2,2,32,2560]{3,2,1,0:T(8,128)(2,1)} custom-call(bf16[2,2,32,2560]{3,2,1,0:T(8,128)(2,1)} %x_ref.1, f32[4,2560]{1,0:T(4,128)} %bitcast.27, bf16[160,2560]{1,0:T(8,128)(2,1)} %bitcast.23, bf16[160,2560]{1,0:T(8,128)(2,1)} %bitcast.24, bf16[160,2560]{1,0:T(8,128)(2,1)} %bitcast.25, bf16[160,2560]{1,0:T(8,128)(2,1)} %bitcast.26, ...), custom_call_target="tpu_custom_call" | custom-call | tf_op jit(solution)/shard_map/pipeline/pallas_call | solution.py:391
  395.8 2.0 copy.12
